TPU v7x, 32 devices: a whole 2x2x4 slice. The times are simulated.
32 devices in a mesh: dp: 16 (over z, x, core), tensor: 2 (over y).
Axes of the slice: x: 2, y: 2, z: 4, core: 2. Of those that a mesh axis runs over, the one named last changes fastest.
Arguments:
- residual: bfloat16 [4096, 4096], P('dp', 'tensor'), may hold values from -6 to 6
- fresh_qkv: bfloat16 [4096, 3, 2048], P('dp', None, 'tensor'), may hold values from -110 to 110
- active: int32 [4096], P('dp'), may hold values from 0 to 1
- home_slot: int32 [4096], P('dp'), may hold values from 0 to 4095, as said below
- kv_cache: bfloat16 [4096, 2, 16, 2048], P('dp', None, None, 'tensor'), may hold values from -6 to 6
- lengths: int32 [4096], P('dp'), may hold values from 2 to 16
- w_out: bfloat16 [2048, 4096], P('tensor'), may hold values from -0.125 to 0.125
Outputs:
- updated: bfloat16 [4096, 4096], P('dp', 'tensor')
Inputs may be any that keep to these rules, and one draw needn't show every extreme that they name: Each dp group owns the slots 256 * g to 256 * g + 255; home_slot is a permutation. Among the streams of one dp group, at most 16 active streams have slots in the same owning group, and this is reached in every draw.
All inputs are finite; a program needn't handle non-finite values.
Results may differ from a plain program's by a relative error of at most 0.0062.
Values may be sent and summed in bfloat16 or wider, within the bound.
No kernel may reach another device: no remote copies, remote signals or barrier semaphores. Data moves between devices by JAX's collectives and lax.ppermute only.
A program may use at most 128 MiB of HBM per device.

v0:
```python
import jax
import jax.numpy as jnp
from jax import lax
from jax.sharding import PartitionSpec as P

HD = 128


def attend_local(fresh_rows, kv_cache, lengths, heads_local):
    streams_here = fresh_rows.shape[0]
    cache_len = kv_cache.shape[2]
    head_size = fresh_rows.shape[1] // (3 * heads_local)
    score_scale = head_size ** (-0.5)
    fresh_split = fresh_rows.reshape(streams_here, 3, heads_local, head_size)
    query = fresh_split[:, 0]
    key_rows = kv_cache[:, 0].reshape(streams_here, cache_len, heads_local, head_size)
    value_rows = kv_cache[:, 1].reshape(streams_here, cache_len, heads_local, head_size)
    scores = (
        jnp.einsum("bhd,blhd->bhl", query, key_rows, preferred_element_type=jnp.float32)
        * score_scale
    )
    positions = jnp.arange(cache_len, dtype=jnp.int32)
    in_cache = positions[None, None, :] < lengths[:, None, None]
    scores = jnp.where(in_cache, scores, jnp.float32(-1e30))
    own_score = (
        jnp.sum(query.astype(jnp.float32) * fresh_split[:, 1].astype(jnp.float32), axis=-1)
        * score_scale
    )
    row_max = jnp.maximum(jnp.max(scores, axis=-1), own_score)
    weights_raw = jnp.exp(scores - row_max[..., None])
    own_raw = jnp.exp(own_score - row_max)
    denominator = jnp.sum(weights_raw, axis=-1) + own_raw
    weights = (weights_raw / denominator[..., None]).astype(jnp.bfloat16)
    own_weight = (own_raw / denominator).astype(jnp.bfloat16)
    mixed = jnp.einsum("bhl,blhd->bhd", weights, value_rows, preferred_element_type=jnp.float32)
    mixed = mixed + own_weight.astype(jnp.float32)[..., None] * fresh_split[:, 2].astype(
        jnp.float32
    )
    return mixed.astype(jnp.bfloat16).reshape(streams_here, heads_local * head_size)


def body(residual, fresh_qkv, active, home_slot, kv_cache, lengths, w_out):
    groups = lax.axis_size("dp")
    group_here = lax.axis_index("dp")
    streams_here = home_slot.shape[0]
    width_here = fresh_qkv.shape[2]
    heads_local = width_here // HD
    capacity = max(2, streams_here // groups)
    slot_count = groups * capacity
    owner_group = home_slot // streams_here
    is_active = active > 0
    earlier = jnp.arange(streams_here)[:, None] < jnp.arange(streams_here)[None, :]
    same_owner = (
        (owner_group[:, None] == owner_group[None, :])
        & is_active[:, None]
        & is_active[None, :]
        & earlier
    )
    send_rank = jnp.sum(same_owner.astype(jnp.int32), axis=0)
    target = owner_group * capacity + send_rank
    placed = (jnp.arange(slot_count, dtype=jnp.int32)[:, None] == target[None, :]) & is_active[
        None, :
    ]
    placing = placed.astype(jnp.bfloat16)
    fresh_flat = fresh_qkv.reshape(streams_here, 3 * width_here)
    send_rows = jnp.dot(placing, fresh_flat, preferred_element_type=jnp.float32).astype(
        jnp.bfloat16
    )
    send_rows = send_rows.reshape(groups, capacity, 3 * width_here)
    slot_ids = jnp.sum(jnp.where(placed, home_slot[None, :] + 1, 0), axis=1) - 1
    slot_ids = slot_ids.reshape(groups, capacity)
    got_rows, got_ids = (
        lax.all_to_all(send_rows, "dp", split_axis=0, concat_axis=0, tiled=True),
        lax.all_to_all(slot_ids, "dp", split_axis=0, concat_axis=0, tiled=True),
    )
    local_slot = got_ids.reshape(slot_count) - group_here * streams_here
    matched = (local_slot[None, :] == jnp.arange(streams_here, dtype=jnp.int32)[:, None]).astype(
        jnp.bfloat16
    )
    owned = jnp.dot(
        matched, got_rows.reshape(slot_count, 3 * width_here), preferred_element_type=jnp.float32
    ).astype(jnp.bfloat16)
    attended = attend_local(owned, kv_cache, lengths, heads_local)
    heads_rows = jnp.dot(matched.T, attended, preferred_element_type=jnp.float32).astype(
        jnp.bfloat16
    )
    returned = lax.all_to_all(
        heads_rows.reshape(groups, capacity, width_here),
        "dp",
        split_axis=0,
        concat_axis=0,
        tiled=True,
    )
    source_rows = jnp.dot(
        placing.T, returned.reshape(slot_count, width_here), preferred_element_type=jnp.float32
    ).astype(jnp.bfloat16)
    partial_rows = jnp.dot(source_rows, w_out, preferred_element_type=jnp.float32)
    gained = lax.psum_scatter(partial_rows, "tensor", scatter_dimension=1, tiled=True)
    return (residual.astype(jnp.float32) + gained).astype(jnp.bfloat16)


def solution(mesh):
    placed = (
        P("dp", "tensor"),
        P("dp", None, "tensor"),
        P("dp"),
        P("dp"),
        P("dp", None, None, "tensor"),
        P("dp"),
        P("tensor", None),
    )
    return jax.shard_map(
        body, mesh=mesh, in_specs=placed, out_specs=P("dp", "tensor"), check_vma=False
    )
```

profile of v0, /device:TPU:0, one launch (start us, length us, event | category | flops | bytes accessed | tf_op | source)
XLA Modules:
  0.0 170.8 jit_solution(18366352465075356929)
XLA Ops:
  6.5 0.7 broadcast_add_fusion.1
  7.2 0.7 broadcast_compare_fusion
  7.9 0.2 convert_reduce_fusion
  8.1 0.1 select_reduce_fusion
  8.2 0.7 sub.45
  8.9 7.4 %all-to-all-start = ((s32[16,1,16]{2,1,0:T(1,128)}), s32[16,1,16]{2,1,0:T(1,128)S(1)}, u32[]{:S(2)}, u32[]{:S(2)}) async-start(s32[16,1,16]{2,1,0:T(1,128)} %sub.45), calls=%async_computation | async-start | bytes 16384 | tf_op jit(solution)/shard_map/all_to_all | solution.py:74
  16.3 1.7 copy.14
  18.0 1.8 %convolution_convert_fusion.1 = bf16[256,3072]{1,0:T(8,128)(2,1)} fusion(bf16[256,3072]{0,1:T(8,128)(2,1)S(1)} %bitcast.71, s32[256]{0:T(256)S(1)} %multiply_add_fusion, pred[256]{0:T(512)(128)(4,1)S(1)} %broadcast_compare_fusion), kind=kOutput, calls=%fused_computation.5 | convolution fusion | flops 403570688 | bytes 3147008 | tf_op jit(solution)/shard_map/dot_general | solution.py:66
  19.9 2.8 %all-to-all-done = s32[16,1,16]{2,1,0:T(1,128)S(1)} async-done(((s32[16,1,16]{2,1,0:T(1,128)}), s32[16,1,16]{2,1,0:T(1,128)S(1)}, u32[]{:S(2)}, u32[]{:S(2)}) %all-to-all-start) | async-done | bytes 1056 | tf_op jit(solution)/shard_map/all_to_all | solution.py:74
  22.7 3.7 %all-to-all-start.1 = ((bf16[16,16,3072]{2,1,0:T(8,128)(2,1)}), bf16[16,16,3072]{2,1,0:T(8,128)(2,1)S(1)}, u32[]{:S(2)}, u32[]{:S(2)}) async-start(bf16[16,16,3072]{2,1,0:T(8,128)(2,1)} %bitcast.1), calls=%async_computation.1 | async-start | bytes 3145728 | tf_op jit(solution)/shard_map/all_to_all | solution.py:73
  26.4 0.0 reduce-scatter.2.cloned.1.call-start
  26.4 12.4 %fusion.31 = (bf16[256,1,16,1024]{3,2,1,0:T(8,128)(2,1)}, bf16[256,1,16,1024]{3,2,1,0:T(8,128)(2,1)}) fusion(bf16[256,2,16,1024]{3,2,1,0:T(8,128)(2,1)} %param.11), kind=kLoop, calls=%fused_computation.57 | loop fusion | bytes 33554432 | tf_op jit(solution)/shard_map/slice | solution.py:17
  38.8 8.8 %copy.28 = bf16[512,8,8,128]{3,2,1,0:T(8,128)(2,1)} copy(bf16[512,8,8,128]{3,1,2,0:T(8,128)(2,1)} %bitcast.64) | data formatting | bytes 16777216
  47.6 0.0 copy-start.1
  47.6 8.8 %copy.29 = bf16[512,8,8,128]{3,2,1,0:T(8,128)(2,1)} copy(bf16[512,8,8,128]{3,1,2,0:T(8,128)(2,1)} %bitcast.63) | data formatting | bytes 16777216
  56.4 0.0 copy-done.1
  56.4 0.1 sub.48
  56.5 1.6 all-to-all-done.1
  58.2 0.6 fusion.4
  58.8 0.3 copy.27
  59.1 0.3 fusion.8
  59.5 0.1 copy.17
  59.5 7.8 %fusion.2 = f32[256,8,1,16]{3,2,1,0:T(1,128)S(1)} fusion(bf16[256,16,8,128]{3,2,1,0:T(8,128)(2,1)} %bitcast.69, bf16[256,8,128,1]{2,1,0,3:T(8,128)(2,1)S(1)} %slice_bitcast_fusion.2), kind=kOutput, calls=%fused_computation.2 | convolution fusion | flops 8388608 | bytes 9043968 | tf_op jit(solution)/shard_map/bhd,blhd->bhl/dot_general | solution.py:19
  67.3 0.8 copy.21
  68.3 1.1 copy.22
  69.4 0.1 copy.18
  69.6 5.7 %fusion = f32[256,8,1,128]{3,2,1,0:T(1,128)S(1)} fusion(bf16[256,8,16,1]{2,3,1,0:T(2,128)(2,1)S(1)} %copy.22, bf16[256,16,8,128]{3,2,1,0:T(8,128)(2,1)} %bitcast.68), kind=kOutput, calls=%fused_computation | convolution fusion | flops 8388608 | bytes 9502720 | tf_op jit(solution)/shard_map/bhl,blhd->bhd/dot_general | solution.py:35
  75.3 0.4 fusion.7
  75.6 0.3 convolution_convert_fusion.3
  76.0 23.1 %all_to_all.16 = bf16[16,16,1024]{2,1,0:T(8,128)(2,1)S(1)} all-to-all(bf16[16,16,1024]{2,1,0:T(8,128)(2,1)S(1)} %bitcast.73), channel_id=1, replica_groups=mesh['dp'=16,'tensor'=2] {'dp'}, dimensions={0} | all-to-all | bytes 1048576 | tf_op jit(solution)/shard_map/all_to_all | solution.py:87
  99.1 7.8 %fusion.5 = f32[256,4096]{1,0:T(8,128)} fusion(bf16[1024,4096]{1,0:T(8,128)(2,1)} %param.13, bf16[256,1024]{1,0:T(8,128)(2,1)S(1)} %bitcast.75, s32[256]{0:T(256)S(1)} %multiply_add_fusion, pred[256]{0:T(512)(128)(4,1)S(1)} %broadcast_compare_fusion), kind=kOutput, calls=%fused_computation.10 | convolution fusion | flops 2282094592 | bytes 13108480 | tf_op jit(solution)/shard_map/dot_general | solution.py:97
  106.9 0.0 copy-start
  107.0 0.0 reduce-scatter.2.cloned.1.call-update
  107.0 54.1 %reduce-scatter.2.cloned.1.call-done = f32[256,2048]{1,0:T(8,128)} async-done(((f32[256,4096]{1,0:T(8,128)}), f32[256,2048]{1,0:T(8,128)}) %reduce-scatter.2.cloned.1.call-update) | async-done | bytes 2097168 | tf_op jit(solution)/shard_map/reduce_scatter | solution.py:98
  161.1 0.0 copy-done
  161.1 2.8 %add_convert_fusion = bf16[256,2048]{1,0:T(8,128)(2,1)} fusion(f32[256,2048]{1,0:T(8,128)} %reduce-scatter.2.cloned.1.call-done, bf16[256,2048]{1,0:T(8,128)(2,1)S(1)} %copy-done), kind=kLoop, calls=%fused_computation.6 | loop fusion | flops 1572864 | bytes 4194304 | tf_op jit(solution)/shard_map/convert_element_type | solution.py:99
  (10 shorter events, 0.2 us)
Async XLA Ops:
  8.9 13.8 %all-to-all-start = ((s32[16,1,16]{2,1,0:T(1,128)}), s32[16,1,16]{2,1,0:T(1,128)S(1)}, u32[]{:S(2)}, u32[]{:S(2)}) async-start(s32[16,1,16]{2,1,0:T(1,128)} %sub.45), calls=%async_computation | async-start | bytes 16384 | tf_op jit(solution)/shard_map/all_to_all | solution.py:74
  22.7 35.5 %all-to-all-start.1 = ((bf16[16,16,3072]{2,1,0:T(8,128)(2,1)}), bf16[16,16,3072]{2,1,0:T(8,128)(2,1)S(1)}, u32[]{:S(2)}, u32[]{:S(2)}) async-start(bf16[16,16,3072]{2,1,0:T(8,128)(2,1)} %bitcast.1), calls=%async_computation.1 | async-start | bytes 3145728 | tf_op jit(solution)/shard_map/all_to_all | solution.py:73
  26.4 134.7 %reduce-scatter.2.cloned.1.call-start = ((), (), s32[]{:S(2)}) async-start(), calls=%async_computation.4 | async-start | bytes 6291456 | tf_op jit(solution)/shard_map/reduce_scatter | solution.py:98
  47.6 8.8 %copy-start.1 = (s32[256]{0:T(256)S(1)}, s32[256]{0:T(256)}, u32[]{:S(2)}) copy-start(s32[256]{0:T(256)} %param.12) | copy-start | bytes 3076
  106.9 54.1 %copy-start = (bf16[256,2048]{1,0:T(8,128)(2,1)S(1)}, bf16[256,2048]{1,0:T(8,128)(2,1)}, u32[]{:S(2)}) copy-start(bf16[256,2048]{1,0:T(8,128)(2,1)} %param.7) | copy-start | bytes 3145732
Sparse Core Ops, SparseCore 0:
  107.1 53.9 reduce-scatter.1
where the time goes:
time: 171 us
  waiting for transfers between devices  58.5 us (34%)
  local copies, waits for them, and re-layouts  34.9 us (20%)
  matrix products  24.1 us (14%)
  blocking collectives  23.1 us (14%)
  between operations  13.6 us (8%)
  starting transfers between devices  11.1 us (6%)
  other arithmetic  5.39 us (3%)
    reduce_scatter x1, waiting for transfers between devices, body(): lax.psum_scatter(partial_rows, 'tensor', scatter_dimension=1, tiled=True)  54.1 us
    all_to_all x1, blocking collectives, body(): lax.all_to_all(heads_rows.reshape(groups, capacity, width_here), 'dp', sp...  23.1 us
    unnamed x8, local copies, waits for them, and re-layouts  19.6 us
    slice x1, local copies, waits for them, and re-layouts, attend_local(): kv_cache[:, 1].reshape(streams_here, cache_len, heads_local, head_size)  12.4 us
    dot_general x1, matrix products, body(): jnp.dot(source_rows, w_out, preferred_element_type=jnp.float32)  7.83 us
    dot_general x1, matrix products, attend_local(): jnp.einsum('bhd,blhd->bhl', query, key_rows, preferred_element_type=jnp.f...  7.8 us
    all_to_all x1, starting transfers between devices, body(): lax.all_to_all(slot_ids, 'dp', split_axis=0, concat_axis=0, tiled=True)  7.39 us
    dot_general x1, matrix products, attend_local(): jnp.einsum('bhl,blhd->bhd', weights, value_rows, preferred_element_type=j...  5.69 us
  transfers between devices with their start and end apart: 3, of which 3 were waited for; matrix products, arithmetic and copies ran while one was open for 20% of the time, Pallas kernels for 0%

commit v1 on v0

v1 whole, which is shorter than its diff:
```python
import functools

import jax
import jax.numpy as jnp
from jax import lax
from jax.experimental import pallas as pl
from jax.experimental.pallas import tpu as pltpu
from jax.sharding import PartitionSpec as P

HD = 128
LANES = 128
ID_BASE = 128
F32 = jnp.float32
BF16 = jnp.bfloat16


def vmem():
    return pl.BlockSpec(memory_space=pltpu.VMEM)


def dot(a, b, dims=((1,), (0,))):
    return lax.dot_general(a, b, (dims, ((), ())), preferred_element_type=F32)


def cost(flops, bytes_accessed):
    return pl.CostEstimate(flops=flops, bytes_accessed=bytes_accessed, transcendentals=0)


def route_kernel(streams, capacity, home_ref, active_ref, query_ref, send_ref, placing_ref):
    rows = send_ref.shape[0]
    width = query_ref.shape[1]
    home = home_ref[...]
    is_active = active_ref[...] > 0
    owner = home // streams
    code_row = jnp.where(is_active, owner, -1).astype(F32)
    code_col = jnp.transpose(jnp.broadcast_to(code_row, (streams, streams)))
    before = lax.broadcasted_iota(jnp.int32, (streams, streams), 0) < lax.broadcasted_iota(
        jnp.int32, (streams, streams), 1
    )
    rank = jnp.sum(
        jnp.where((code_col == code_row) & before, 1.0, 0.0), axis=0, keepdims=True
    ).astype(jnp.int32)
    target = jnp.where(is_active, owner * capacity + rank, -1)
    placing = jnp.where(
        lax.broadcasted_iota(jnp.int32, (rows, streams), 0) == target, 1.0, 0.0
    ).astype(BF16)
    placing_ref[...] = placing
    send_ref[:, :width] = dot(placing, query_ref[...]).astype(BF16)
    local = home - owner * streams
    kind = lax.broadcasted_iota(jnp.int32, (LANES, streams), 0)
    ids = jnp.where(
        kind == 0, local // ID_BASE, jnp.where(kind == 1, local % ID_BASE, jnp.where(kind == 2, 1, 0))
    )
    send_ref[:, width:] = dot(placing, ids.astype(F32).astype(BF16), ((1,), (1,))).astype(BF16)


def route(home, active, query, capacity, groups):
    streams, width = query.shape
    rows = groups * capacity
    return pl.pallas_call(
        functools.partial(route_kernel, streams, capacity),
        out_shape=(
            jax.ShapeDtypeStruct((rows, width + LANES), BF16),
            jax.ShapeDtypeStruct((rows, streams), BF16),
        ),
        in_specs=[vmem()] * 3,
        out_specs=(vmem(), vmem()),
        cost_estimate=cost(2 * rows * streams * (width + LANES), 4 * streams * width),
        name="route",
    )(home.reshape(1, streams), active.reshape(1, streams), query)


def attend_kernel(heads, block, pair, got_ref, bias_ref, kv_ref, back_ref, owned_ref, mixed_ref):
    step = pl.program_id(0)
    rows, padded = got_ref.shape
    slots = owned_ref.shape[0]
    cache_len = kv_ref.shape[2]
    width = heads * HD
    scale = HD ** (-0.5)

    def matched():
        tail = got_ref[:, width:].astype(F32)
        local = (tail[:, 0:1] * ID_BASE + tail[:, 1:2]).astype(jnp.int32)
        local = jnp.where(tail[:, 2:3] > 0, local, -1)
        lanes = lax.broadcasted_iota(jnp.int32, (rows, slots), 1)
        return jnp.where(lanes == local, 1.0, 0.0).astype(BF16)

    @pl.when(step == 0)
    def _():
        owned_ref[...] = dot(matched(), got_ref[:, :width], ((0,), (0,))).astype(BF16)

    per_step = kv_ref.shape[0] // block
    span = block * cache_len
    same_slot = (
        lax.broadcasted_iota(jnp.int32, (pair * block, span), 0) % block
        == lax.broadcasted_iota(jnp.int32, (pair * block, span), 1) // cache_len
    )
    head_of_row = lax.broadcasted_iota(jnp.int32, (pair * block, pair * HD), 0) // block
    head_of_lane = lax.broadcasted_iota(jnp.int32, (pair * block, pair * HD), 1) // HD
    same_head = head_of_row == head_of_lane
    lanes = lax.broadcasted_iota(jnp.int32, (block, LANES), 1)
    for i in range(per_step):
        start = pl.multiple_of((step * per_step + i) * block, block)
        bias = bias_ref[pl.ds(step * per_step + i, 1), :]
        sums = jnp.where(lanes == 3 * heads, 1.0, 0.0)
        for j in range(heads // pair):
            cols = slice(j * pair * HD, (j + 1) * pair * HD)
            query = owned_ref[pl.ds(start, block), cols]
            spread = jnp.where(same_head, jnp.concatenate([query] * pair, axis=0), 0).astype(BF16)
            keys = kv_ref[i * block:(i + 1) * block, 0, :, cols].reshape(span, pair * HD)
            values = kv_ref[i * block:(i + 1) * block, 1, :, cols].reshape(span, pair * HD)
            scores = dot(spread, keys, ((1,), (1,))) * scale
            scores = jnp.where(same_slot, scores + bias, -jnp.inf)
            top = jnp.max(scores, axis=1, keepdims=True)
            raw = jnp.exp(scores - top)
            total = jnp.sum(raw, axis=1, keepdims=True)
            mixed = dot(raw.astype(BF16), values) / total
            log_sum = top + jnp.log(total)
            for k in range(pair):
                h = j * pair + k
                mixed_ref[pl.ds(start, block), h * HD:(h + 1) * HD] = mixed[
                    k * block:(k + 1) * block, k * HD:(k + 1) * HD
                ].astype(BF16)
                part = log_sum[k * block:(k + 1) * block, :]
                high = part.astype(BF16).astype(F32)
                middle = (part - high).astype(BF16).astype(F32)
                low = (part - high) - middle
                sums = jnp.where(lanes == h, high, sums)
                sums = jnp.where(lanes == heads + h, middle, sums)
                sums = jnp.where(lanes == 2 * heads + h, low, sums)
        mixed_ref[pl.ds(start, block), width:] = sums.astype(BF16)

    @pl.when(step == pl.num_programs(0) - 1)
    def _():
        back_ref[...] = dot(matched(), mixed_ref[...]).astype(BF16)


def attend(got, kv_cache, lengths, block, per_step):
    rows, padded = got.shape
    width = padded - LANES
    heads = width // HD
    slots, _, cache_len, _ = kv_cache.shape
    pair = 2 if heads % 2 == 0 else 1
    bias = jnp.where(
        jnp.arange(cache_len, dtype=jnp.int32)[None, :] < lengths[:, None], F32(0), F32(-1e30)
    ).reshape(slots // block, block * cache_len)
    step_slots = block * per_step
    return pl.pallas_call(
        functools.partial(attend_kernel, heads, block, pair),
        grid=(slots // step_slots,),
        out_shape=jax.ShapeDtypeStruct((rows, padded), BF16),
        in_specs=[
            pl.BlockSpec((rows, padded), lambda i: (0, 0)),
            pl.BlockSpec(bias.shape, lambda i: (0, 0)),
            pl.BlockSpec((step_slots, 2, cache_len, width), lambda i: (i, 0, 0, 0)),
        ],
        out_specs=pl.BlockSpec((rows, padded), lambda i: (0, 0)),
        scratch_shapes=[pltpu.VMEM((slots, width), BF16), pltpu.VMEM((slots, padded), BF16)],
        compiler_params=pltpu.CompilerParams(dimension_semantics=("arbitrary",)),
        cost_estimate=cost(4 * rows * slots * padded, 2 * kv_cache.size),
        name="attend",
    )(got, bias, kv_cache)


def merge_kernel(heads, back_ref, placing_ref, fresh_ref, out_ref):
    width = heads * HD
    scale = HD ** (-0.5)
    rows = dot(placing_ref[...], back_ref[...], ((0,), (0,)))
    tail = rows[:, width:]
    valid = tail[:, 3 * heads:3 * heads + 1] > 0
    for h in range(heads):
        cols = slice(h * HD, (h + 1) * HD)
        query, key, value = (fresh_ref[k, :, cols].astype(F32) for k in range(3))
        own = jnp.sum(query * key, axis=1, keepdims=True) * scale
        log_sum = (
            tail[:, h:h + 1] + tail[:, heads + h:heads + h + 1]
        ) + tail[:, 2 * heads + h:2 * heads + h + 1]
        top = jnp.maximum(own, log_sum)
        cached_raw = jnp.exp(log_sum - top)
        own_raw = jnp.exp(own - top)
        total = cached_raw + own_raw
        mixed = (cached_raw / total) * rows[:, cols] + (own_raw / total) * value
        out_ref[:, cols] = jnp.where(valid, mixed, 0.0).astype(BF16)


def merge(back, placing, fresh):
    streams, width = fresh.shape[1:]
    return pl.pallas_call(
        functools.partial(merge_kernel, width // HD),
        out_shape=jax.ShapeDtypeStruct((streams, width), BF16),
        in_specs=[vmem()] * 3,
        out_specs=vmem(),
        cost_estimate=cost(2 * streams * back.size, 2 * (back.size + fresh.size)),
        name="merge",
    )(back, placing, fresh)


def own_kernel(where_ref, rows_ref, w_ref, residual_ref, out_ref):
    out_ref[...] = residual_ref[...].astype(F32) + dot(rows_ref[...], w_ref[...])


def project_own(rows, w_out, residual, place, tile):
    streams, width = rows.shape
    out_cols = residual.shape[1]
    tiles = out_cols // tile
    return pl.pallas_call(
        own_kernel,
        grid_spec=pltpu.PrefetchScalarGridSpec(
            num_scalar_prefetch=1,
            grid=(tiles,),
            in_specs=[
                pl.BlockSpec((streams, width), lambda i, p: (0, 0)),
                pl.BlockSpec((width, tile), lambda i, p: (0, p[0] * tiles + i)),
                pl.BlockSpec((streams, tile), lambda i, p: (0, i)),
            ],
            out_specs=pl.BlockSpec((streams, tile), lambda i, p: (0, i)),
        ),
        out_shape=jax.ShapeDtypeStruct((streams, out_cols), F32),
        cost_estimate=cost(2 * rows.size * out_cols, 2 * width * out_cols),
        name="project_own",
    )(place, rows, w_out, residual)


def rest_kernel(count, where_ref, sum_ref, *refs):
    out_ref = refs[-1]
    half = refs[1].shape[0]
    mine = pl.multiple_of(where_ref[1] * half, half)
    other = pl.multiple_of((1 - where_ref[1]) * half, half)
    total = sum_ref[...]
    for k in range(count):
        rows_ref, first_ref, second_ref = refs[3 * k:3 * k + 3]
        total += dot(rows_ref[:, pl.ds(mine, half)], first_ref[...])
        total += dot(rows_ref[:, pl.ds(other, half)], second_ref[...])
    out_ref[...] = total.astype(out_ref.dtype)


def project_rest(partial, pieces, place, tile):
    streams, out_cols = partial.shape
    specs, operands = [], []
    for rows, first, second in pieces:
        specs += [
            pl.BlockSpec(rows.shape, lambda i, p: (0, 0)),
            pl.BlockSpec((first.shape[0], tile), lambda i, p: (0, i)),
            pl.BlockSpec((second.shape[0], tile), lambda i, p: (0, i)),
        ]
        operands += [rows, first, second]
    return pl.pallas_call(
        functools.partial(rest_kernel, len(pieces)),
        grid_spec=pltpu.PrefetchScalarGridSpec(
            num_scalar_prefetch=1,
            grid=(out_cols // tile,),
            in_specs=[pl.BlockSpec((streams, tile), lambda i, p: (0, i))] + specs,
            out_specs=pl.BlockSpec((streams, tile), lambda i, p: (0, i)),
        ),
        out_shape=jax.ShapeDtypeStruct((streams, out_cols), BF16),
        cost_estimate=cost(2 * streams * out_cols * 1024, 4 * streams * out_cols),
        name="project_rest",
    )(place, partial, *operands)


def body(residual, fresh_qkv, active, home_slot, kv_cache, lengths, w_out):
    groups = lax.axis_size("dp")
    parts = lax.axis_size("tensor")
    group_here = lax.axis_index("dp")
    part_here = lax.axis_index("tensor")
    streams = home_slot.shape[0]
    width = fresh_qkv.shape[2]
    capacity = max(2, streams // groups)
    out_cols = residual.shape[1]
    half = width // 2
    core = group_here % 2
    place = jnp.stack([part_here, core]).astype(jnp.int32)

    swap = [(i, i ^ 1) for i in range(groups)]
    weights = []
    for k in range(1, parts):
        ring = [(i, (i + k) % parts) for i in range(parts)]
        to = (part_here + k) % parts
        block = lax.dynamic_slice(w_out, (core * half, to * out_cols), (half, out_cols))
        first = lax.ppermute(block, "tensor", ring)
        second = lax.ppermute(first, "dp", swap)
        weights.append((ring, first, second))

    fresh = jnp.transpose(fresh_qkv, (1, 0, 2))
    send, placing = route(home_slot, active, fresh[0], capacity, groups)
    padded = width + LANES

    def exchange(rows):
        rows = rows.reshape(groups, capacity, padded)
        rows = lax.all_to_all(rows, "dp", split_axis=0, concat_axis=0, tiled=True)
        return rows.reshape(groups * capacity, padded)

    back = attend(exchange(send), kv_cache, lengths, 16, 4)
    rows = merge(exchange(back), placing, fresh)
    pieces = [
        (lax.ppermute(rows, "tensor", ring), first, second) for ring, first, second in weights
    ]
    partial = project_own(rows, w_out, residual, place, min(512, out_cols))
    return project_rest(partial, pieces, place, min(512, out_cols))


def solution(mesh):
    placed = (
        P("dp", "tensor"),
        P("dp", None, "tensor"),
        P("dp"),
        P("dp"),
        P("dp", None, None, "tensor"),
        P("dp"),
        P("tensor", None),
    )
    return jax.shard_map(
        body, mesh=mesh, in_specs=placed, out_specs=P("dp", "tensor"), check_vma=False
    )
```

time: 171 us -> 125 us (0.73)
  Pallas kernels: 0 us -> 41.1 us
  local copies, waits for them, and re-layouts: 34.9 us -> 6.93 us
  matrix products: 24.1 us -> 0 us
  waiting for transfers between devices: 58.5 us -> 41.5 us
  between operations: 13.6 us -> 0.05 us
  other arithmetic: 5.39 us -> 1.21 us
    reduce_scatter x1 -> x0, waiting for transfers between devices: 54.1 us -> none  [body(): lax.psum_scatter(partial_rows, 'tensor', scatter_dimension=1, tiled=True)]
    ppermute x0 -> x3, waiting for transfers between devices: none -> 41.5 us  [the longest x1 35.6 us: body(): first = lax.ppermute(block, 'tensor', ring)]
    pallas_call x0 -> x5, Pallas kernels: none -> 41.1 us  [the longest x1 22.2 us: attend(): pl.pallas_call(functools.partial(attend_kernel, heads, block, pair), grid...]
    dot_general x6 -> x0, matrix products: 24.1 us -> none  [the longest x1 7.83 us: body(): jnp.dot(source_rows, w_out, preferred_element_type=jnp.float32)]
    unnamed x8, local copies, waits for them, and re-layouts: 19.6 us -> 2.96 us
    slice x1 -> x0, local copies, waits for them, and re-layouts: 12.4 us -> none  [attend_local(): kv_cache[:, 1].reshape(streams_here, cache_len, heads_local, head_size)]
    all_to_all x2 -> x1, starting transfers between devices: 11.1 us -> 5.91 us  [exchange(): rows = lax.all_to_all(rows, 'dp', split_axis=0, concat_axis=0, tiled=True)]
    ppermute x0 -> x3, starting transfers between devices: none -> 4.59 us  [the longest x1 3.06 us: body(): first = lax.ppermute(block, 'tensor', ring)]
  transfers between devices with their start and end apart: 3 -> 4, of which waited for: 3 -> 2; matrix products, arithmetic and copies ran while one was open for 20% -> 3% of each run, Pallas kernels for 0% -> 28%
where the time goes in v1:
time: 125 us
  waiting for transfers between devices  41.5 us (33%)
  Pallas kernels  41.1 us (33%)
  blocking collectives  23.6 us (19%)
  starting transfers between devices  10.5 us (8%)
  local copies, waits for them, and re-layouts  6.93 us (6%)
    ppermute x1, waiting for transfers between devices, body(): first = lax.ppermute(block, 'tensor', ring)  35.6 us
    all_to_all x1, blocking collectives, exchange(): rows = lax.all_to_all(rows, 'dp', split_axis=0, concat_axis=0, tiled=True)  23.6 us
    pallas_call x1, Pallas kernels, attend(): pl.pallas_call(functools.partial(attend_kernel, heads, block, pair), grid...  22.2 us
    pallas_call x1, Pallas kernels, project_rest(): pl.pallas_call(functools.partial(rest_kernel, len(pieces)), grid_spec=plt...  6.13 us
    pallas_call x1, Pallas kernels, project_own(): pl.pallas_call(own_kernel, grid_spec=pltpu.PrefetchScalarGridSpec(num_sca...  6.09 us
    ppermute x1, waiting for transfers between devices, body(): lax.ppermute(rows, 'tensor', ring)  5.93 us
    all_to_all x1, starting transfers between devices, exchange(): rows = lax.all_to_all(rows, 'dp', split_axis=0, concat_axis=0, tiled=True)  5.91 us
    pallas_call x1, Pallas kernels, merge(): pl.pallas_call(functools.partial(merge_kernel, width // HD), out_shape=ja...  4.3 us
  transfers between devices with their start and end apart: 4, of which 2 were waited for; matrix products, arithmetic and copies ran while one was open for 3% of the time, Pallas kernels for 28%

profile of v1, /device:TPU:0, one launch (start us, length us, event | category | flops | bytes accessed | tf_op | source)
XLA Modules:
  0.0 124.8 jit_solution(9166901880383053113)
XLA Ops:
  0.0 1.7 %dynamic_slice.3 = bf16[512,2048]{1,0:T(8,128)(2,1)S(1)} dynamic-slice(bf16[1024,4096]{1,0:T(8,128)(2,1)} %w_ref.1, s32[]{:T(128)S(6)} %select_n.24, s32[]{:T(128)S(6)} %select_n.26), dynamic_slice_sizes={512,2048} | dynamic-slice | bytes 4194308 | tf_op jit(solution)/shard_map/dynamic_slice | solution.py:279
  1.7 0.0 copy-start.3
  1.7 3.1 %collective-permute-start.1 = (bf16[512,2048]{1,0:T(8,128)(2,1)S(1)}, bf16[512,2048]{1,0:T(8,128)(2,1)}, u32[]{:S(2)}, u32[]{:S(2)}) collective-permute-start(bf16[512,2048]{1,0:T(8,128)(2,1)S(1)} %dynamic_slice.3), channel_id=1, source_target_pairs={{0,1},{1,0},{2,3},{3,2},{4,5},{5,4},{6,7},{7,6},{8,9},{9,8},{10,11... | collective-permute-start | bytes 6291464 | tf_op jit(solution)/shard_map/ppermute | solution.py:280
  4.8 1.9 %slice_bitcast_fusion.query_ref = bf16[256,1024]{1,0:T(8,128)(2,1)} fusion(bf16[3,256,1024]{2,1,0:T(8,128)(2,1)} %bitcast.11), kind=kLoop, calls=%fused_computation | loop fusion | bytes 1048576 | tf_op jit(solution)/shard_map/squeeze | solution.py:285
  6.7 2.4 %route.1 = (bf16[256,1152]{1,0:T(8,128)(2,1)}, bf16[256,256]{1,0:T(8,128)(2,1)}) custom-call(s32[1,256]{1,0:T(1,128)} %bitcast.17, s32[1,256]{1,0:T(1,128)} %bitcast.18, bf16[256,1024]{1,0:T(8,128)(2,1)} %slice_bitcast_fusion.query_ref), custom_call_target="tpu_custom_call" | custom-call | flops 150994944 | bytes 1048576 | tf_op jit(solution)/shard_map/route/pallas_call | solution.py:60
  9.0 5.9 %all-to-all-start = ((bf16[16,16,1152]{2,1,0:T(8,128)(2,1)}), bf16[16,16,1152]{2,1,0:T(8,128)(2,1)S(1)}, u32[]{:S(2)}, u32[]{:S(2)}) async-start(bf16[16,16,1152]{2,1,0:T(8,128)(2,1)} %bitcast.16), calls=%async_computation | async-start | bytes 1179648 | tf_op jit(solution)/shard_map/all_to_all | solution.py:290
  15.0 35.6 %collective-permute-done.1.refs_1_ = bf16[512,2048]{1,0:T(8,128)(2,1)} collective-permute-done((bf16[512,2048]{1,0:T(8,128)(2,1)S(1)}, bf16[512,2048]{1,0:T(8,128)(2,1)}, u32[]{:S(2)}, u32[]{:S(2)}) %collective-permute-start.1) | collective-permute-done | bytes 2097184 | tf_op jit(solution)/shard_map/ppermute | solution.py:280
  50.5 0.0 collective-permute-start.2
  50.5 0.0 copy-done.3
  50.5 0.1 lt.42
  50.6 0.1 lt.40
  50.7 0.1 lt.43
  50.8 0.1 lt.44
  50.9 0.6 compare_select_fusion.bias_ref
  51.5 0.0 all-to-all-done
  51.5 0.0 copy-start
  51.5 0.8 copy-done
  52.4 22.2 %attend.1 = bf16[256,1152]{1,0:T(8,128)(2,1)} custom-call(bf16[256,1152]{1,0:T(8,128)(2,1)} %bitcast.13, f32[16,256]{1,0:T(8,128)} %compare_select_fusion.bias_ref, bf16[256,2,16,1024]{3,2,1,0:T(8,128)(2,1)} %kv_ref.1), custom_call_target="tpu_custom_call" | custom-call | flops 301989888 | bytes 16777216 | tf_op jit(solution)/shard_map/attend/pallas_call | solution.py:148
  74.6 23.6 %all_to_all.10 = bf16[16,16,1152]{2,1,0:T(8,128)(2,1)} all-to-all(bf16[16,16,1152]{2,1,0:T(8,128)(2,1)} %bitcast.14), channel_id=1, replica_groups=mesh['dp'=16,'tensor'=2] {'dp'}, dimensions={0} | all-to-all | bytes 1179648 | tf_op jit(solution)/shard_map/all_to_all | solution.py:290
  98.1 4.3 %merge.1.rows_ref = bf16[256,1024]{1,0:T(8,128)(2,1)} custom-call(bf16[256,1152]{1,0:T(8,128)(2,1)} %bitcast.15, bf16[256,256]{1,0:T(8,128)(2,1)} %get-tuple-element.8.placing_ref, bf16[3,256,1024]{2,1,0:T(8,128)(2,1)} %bitcast.12), custom_call_target="tpu_custom_call" | custom-call | flops 150994944 | bytes 2162688 | tf_op jit(solution)/shard_map/merge/pallas_call | solution.py:188
  102.4 1.5 %collective-permute-start = (bf16[256,1024]{1,0:T(8,128)(2,1)}, bf16[256,1024]{1,0:T(8,128)(2,1)S(1)}, u32[]{:S(2)}, u32[]{:S(2)}) collective-permute-start(bf16[256,1024]{1,0:T(8,128)(2,1)} %merge.1.rows_ref), channel_id=1, source_target_pairs={{0,1},{1,0},{2,3},{3,2},{4,5},{5,4},{6,7},{7,6},{8,9},{9,8},{10,11... | collective-permute-start | bytes 1572872 | tf_op jit(solution)/shard_map/ppermute | solution.py:296
  103.9 0.6 pad_add_fusion.where_ref
  104.6 6.1 %project_own.1.sum_ref = f32[256,2048]{1,0:T(8,128)} custom-call(s32[2]{0:T(128)} %pad_add_fusion.where_ref, bf16[256,1024]{1,0:T(8,128)(2,1)} %merge.1.rows_ref, bf16[1024,4096]{1,0:T(8,128)(2,1)} %w_ref.1, bf16[256,2048]{1,0:T(8,128)(2,1)} %residual_ref.1), custom_call_target="tpu_custom_call" | custom-call | flops 1073741824 | bytes 4194304 | tf_op jit(solution)/shard_map/project_own/pallas_call | solution.py:206
  110.6 5.9 %collective-permute-done.refs_0_ = bf16[256,1024]{1,0:T(8,128)(2,1)S(1)} collective-permute-done((bf16[256,1024]{1,0:T(8,128)(2,1)}, bf16[256,1024]{1,0:T(8,128)(2,1)S(1)}, u32[]{:S(2)}, u32[]{:S(2)}) %collective-permute-start) | collective-permute-done | bytes 524320 | tf_op jit(solution)/shard_map/ppermute | solution.py:296
  116.6 0.0 copy-start.2
  116.6 0.0 collective-permute-done.2.refs_2_
  116.6 0.8 copy-done.2
  117.4 0.0 copy-start.1
  117.4 1.3 %copy-done.1 = bf16[512,2048]{1,0:T(8,128)(2,1)} copy-done((bf16[512,2048]{1,0:T(8,128)(2,1)}, bf16[512,2048]{1,0:T(8,128)(2,1)S(1)}, u32[]{:S(2)}) %copy-start.1) | copy-done | bytes 2097176
  118.7 6.1 %project_rest.1 = bf16[256,2048]{1,0:T(8,128)(2,1)} custom-call(s32[2]{0:T(128)} %pad_add_fusion.where_ref, f32[256,2048]{1,0:T(8,128)} %project_own.1.sum_ref, bf16[256,1024]{1,0:T(8,128)(2,1)} %copy-done.2, bf16[512,2048]{1,0:T(8,128)(2,1)} %collective-permute-done.1.refs_1_, bf16[512,2048]{1,0:T(8,128)(2,1)} %copy-done.1), custom_call_target="tpu_custom_call" | custom-call | flops 1073741824 | bytes 2097152 | tf_op jit(solution)/shard_map/project_rest/pallas_call | solution.py:247
  (1 shorter events, 0.0 us)
Async XLA Ops:
  1.7 48.8 %copy-start.3 = (s32[256]{0:T(256)S(1)}, s32[256]{0:T(256)}, u32[]{:S(2)}) copy-start(s32[256]{0:T(256)} %param.12) | copy-start | bytes 3076
  1.7 48.8 %collective-permute-start.1 = (bf16[512,2048]{1,0:T(8,128)(2,1)S(1)}, bf16[512,2048]{1,0:T(8,128)(2,1)}, u32[]{:S(2)}, u32[]{:S(2)}) collective-permute-start(bf16[512,2048]{1,0:T(8,128)(2,1)S(1)} %dynamic_slice.3), channel_id=1, source_target_pairs={{0,1},{1,0},{2,3},{3,2},{4,5},{5,4},{6,7},{7,6},{8,9},{9,8},{10,11... | collective-permute-start | bytes 6291464 | tf_op jit(solution)/shard_map/ppermute | solution.py:280
  9.0 42.5 %all-to-all-start = ((bf16[16,16,1152]{2,1,0:T(8,128)(2,1)}), bf16[16,16,1152]{2,1,0:T(8,128)(2,1)S(1)}, u32[]{:S(2)}, u32[]{:S(2)}) async-start(bf16[16,16,1152]{2,1,0:T(8,128)(2,1)} %bitcast.16), calls=%async_computation | async-start | bytes 1179648 | tf_op jit(solution)/shard_map/all_to_all | solution.py:290
  50.5 66.0 %collective-permute-start.2 = (bf16[512,2048]{1,0:T(8,128)(2,1)}, bf16[512,2048]{1,0:T(8,128)(2,1)S(1)}, u32[]{:S(2)}, u32[]{:S(2)}) collective-permute-start(bf16[512,2048]{1,0:T(8,128)(2,1)} %collective-permute-done.1.refs_1_), channel_id=1, source_target_pairs={{0,2},{2,0},{4,6},{6,4},{8,10},{10,8},{12,14},{14,12},{16,18},{18,... | collective-permute-start | bytes 6291464 | tf_op jit(solution)/shard_map/ppermute | solution.py:281
  51.5 0.8 copy-start
  102.4 14.2 %collective-permute-start = (bf16[256,1024]{1,0:T(8,128)(2,1)}, bf16[256,1024]{1,0:T(8,128)(2,1)S(1)}, u32[]{:S(2)}, u32[]{:S(2)}) collective-permute-start(bf16[256,1024]{1,0:T(8,128)(2,1)} %merge.1.rows_ref), channel_id=1, source_target_pairs={{0,1},{1,0},{2,3},{3,2},{4,5},{5,4},{6,7},{7,6},{8,9},{9,8},{10,11... | collective-permute-start | bytes 1572872 | tf_op jit(solution)/shard_map/ppermute | solution.py:296
  116.6 0.8 copy-start.2
  117.4 1.3 %copy-start.1 = (bf16[512,2048]{1,0:T(8,128)(2,1)}, bf16[512,2048]{1,0:T(8,128)(2,1)S(1)}, u32[]{:S(2)}) copy-start(bf16[512,2048]{1,0:T(8,128)(2,1)S(1)} %collective-permute-done.2.refs_2_) | copy-start | bytes 6291460

commit v2 on v0

v2 whole, which is shorter than its diff:
```python
import functools

import jax
import jax.numpy as jnp
from jax import lax
from jax.experimental import pallas as pl
from jax.experimental.pallas import tpu as pltpu
from jax.sharding import PartitionSpec as P


HD = 128
LANES = 128
ID_BASE = 128
F32 = jnp.float32
BF16 = jnp.bfloat16


def vmem():
    return pl.BlockSpec(memory_space=pltpu.VMEM)


def on_chip(*arrays):
    return [pltpu.with_memory_space_constraint(a, pltpu.VMEM) for a in arrays]


def off_chip(*arrays):
    return [pltpu.with_memory_space_constraint(a, pltpu.HBM) for a in arrays]


def limit(mebibytes):
    return pltpu.CompilerParams(vmem_limit_bytes=mebibytes << 20)


def dot(a, b, dims=((1,), (0,))):
    return lax.dot_general(a, b, (dims, ((), ())), preferred_element_type=F32)


def cost(flops, bytes_accessed):
    return pl.CostEstimate(flops=flops, bytes_accessed=bytes_accessed, transcendentals=0)


def place_rows(streams, here, home, active):
    rows = home.shape[1]
    is_active = active > 0
    owner = home // streams
    code_row = jnp.where(is_active, owner, -1).astype(F32)
    code_col = jnp.transpose(jnp.broadcast_to(code_row, (rows, rows)))
    before = lax.broadcasted_iota(jnp.int32, (rows, rows), 0) < lax.broadcasted_iota(
        jnp.int32, (rows, rows), 1
    )
    rank = jnp.sum(
        jnp.where((code_col == code_row) & before, 1.0, 0.0), axis=0, keepdims=True
    ).astype(jnp.int32)
    return owner, owner ^ here, rank, is_active


def one_hot(rows, target):
    hits = lax.broadcasted_iota(jnp.int32, (rows, target.shape[1]), 0) == target
    return jnp.where(hits, 1.0, 0.0).astype(BF16)


def route_kernel(
    capacity, parts, chips, cuts, place_ref, home_ref, active_ref, query_ref, w_ref, *rest
):
    count = len(cuts) * (parts - 1)
    send_refs, block_refs, sems = rest[:-count - 1], rest[-count - 1:-1], rest[-1]
    rows = sum(send_ref.shape[0] for send_ref in send_refs)
    streams, width = query_ref.shape
    copies = []
    for i, block_ref in enumerate(block_refs):
        to = lax.rem(place_ref[0] + i // len(cuts) + 1, parts)
        size, cols = block_ref.shape
        at = cuts[i % len(cuts)][0](place_ref[1], place_ref[3])
        copies.append(
            pltpu.make_async_copy(
                w_ref.at[
                    pl.ds(pl.multiple_of(at, size), size),
                    pl.ds(pl.multiple_of(to * cols, cols), cols),
                ],
                block_ref,
                sems.at[i],
            )
        )
    for copy in copies:
        copy.start()
    home = home_ref[...]
    owner, relative, rank, is_active = place_rows(streams, place_ref[2], home, active_ref[...])
    if chips:
        relative = (relative & 1) * chips + relative // 2
    placing = one_hot(rows, jnp.where(is_active, relative * capacity + rank, -1))
    queries = dot(placing, query_ref[...]).astype(BF16)
    local = home - owner * streams
    kind = lax.broadcasted_iota(jnp.int32, (LANES, streams), 0)
    ids = jnp.where(
        kind == 0, local // ID_BASE, jnp.where(kind == 1, local % ID_BASE, jnp.where(kind == 2, 1, 0))
    )
    ids = dot(placing, ids.astype(F32).astype(BF16), ((1,), (1,))).astype(BF16)
    size = send_refs[0].shape[0]
    for i, send_ref in enumerate(send_refs):
        send_ref[:, :width] = queries[i * size:(i + 1) * size]
        send_ref[:, width:] = ids[i * size:(i + 1) * size]
    for copy in copies:
        copy.wait()


def route(home, active, fresh, w_out, place, capacity, groups, parts, chips, cuts):
    _, streams, width = fresh.shape
    rows = groups * capacity
    blocks = [pltpu.VMEM((size, w_out.shape[1] // parts), BF16) for _, size in cuts] * (parts - 1)
    halves = 2 if chips else 1
    sends = [pltpu.VMEM((rows // halves, width + LANES), BF16)] * halves
    out = pl.pallas_call(
        functools.partial(route_kernel, capacity, parts, chips, cuts),
        grid_spec=pltpu.PrefetchScalarGridSpec(
            num_scalar_prefetch=1,
            grid=(1,),
            in_specs=[
                pl.BlockSpec((1, streams), lambda i, p: (0, 0)),
                pl.BlockSpec((1, streams), lambda i, p: (0, 0)),
                pl.BlockSpec((None, streams, width), lambda i, p: (0, 0, 0)),
                pl.BlockSpec(memory_space=pl.ANY),
            ],
            out_specs=[vmem()] * (halves + len(blocks)),
            scratch_shapes=[pltpu.SemaphoreType.DMA((len(blocks),))],
        ),
        out_shape=sends + blocks,
        cost_estimate=cost(2 * rows * streams * (width + LANES), 4 * streams * width),
        compiler_params=limit(16),
        name="route",
    )(place, *off_chip(home, active, fresh, w_out))
    return out[:halves], out[halves:]


def rows_kernel(
    capacity,
    place_ref,
    home_ref,
    active_ref,
    lengths_ref,
    fresh_hbm,
    cache_hbm,
    placing_ref,
    value_ref,
    own_ref,
    bias_ref,
    cache_ref,
    fresh_ref,
    sems,
):
    pieces = sems.shape[0] - 1
    size = cache_ref.shape[0] // pieces
    first = pltpu.make_async_copy(fresh_hbm, fresh_ref, sems.at[pieces])
    first.start()
    copies = [
        pltpu.make_async_copy(
            cache_hbm.at[pl.ds(i * size, size)], cache_ref.at[pl.ds(i * size, size)], sems.at[i]
        )
        for i in range(pieces)
    ]
    for copy in copies:
        copy.start()
    rows, width = value_ref.shape
    streams = home_ref.shape[1]
    heads = width // HD
    _, relative, rank, is_active = place_rows(streams, place_ref[2], home_ref[...], active_ref[...])
    placing = one_hot(rows, jnp.where(is_active, relative * capacity + rank, -1))
    placing_ref[...] = placing
    first.wait()
    value_ref[...] = dot(placing, fresh_ref[2]).astype(BF16)
    product = dot(placing, fresh_ref[0]) * dot(placing, fresh_ref[1])
    lanes = lax.broadcasted_iota(jnp.int32, own_ref.shape, 1)
    own = jnp.zeros(own_ref.shape, F32)
    for h in range(heads):
        score = jnp.sum(product[:, h * HD:(h + 1) * HD], axis=1, keepdims=True)
        own = jnp.where(lanes == h, score * HD ** (-0.5), own)
    own_ref[...] = own
    blocks, span = bias_ref.shape
    slots = lengths_ref.shape[1]
    block = slots // blocks
    cache_len = span // block
    slot = lax.broadcasted_iota(jnp.int32, (blocks, slots), 1)
    in_block = slot // block == lax.broadcasted_iota(jnp.int32, (blocks, slots), 0)
    length = jnp.where(in_block, lengths_ref[...], 0).astype(F32).astype(BF16)
    slot = lax.broadcasted_iota(jnp.int32, (slots, span), 0)
    spread = slot % block == lax.broadcasted_iota(jnp.int32, (slots, span), 1) // cache_len
    length = dot(length, jnp.where(spread, 1.0, 0.0).astype(BF16))
    position = lax.broadcasted_iota(jnp.int32, bias_ref.shape, 1) % cache_len
    bias_ref[...] = jnp.where(position.astype(F32) < length, 0.0, -1e30)
    for copy in copies:
        copy.wait()


def own_rows(home, active, lengths, fresh, cache, place, capacity, groups, block, pieces=4):
    _, streams, width = fresh.shape
    rows = groups * capacity
    slots, cache_len = cache.shape[0], cache.shape[2]
    whole = pl.BlockSpec(memory_space=pl.ANY)
    return pl.pallas_call(
        functools.partial(rows_kernel, capacity),
        grid_spec=pltpu.PrefetchScalarGridSpec(
            num_scalar_prefetch=1,
            grid=(1,),
            in_specs=[
                pl.BlockSpec((1, streams), lambda i, p: (0, 0)),
                pl.BlockSpec((1, streams), lambda i, p: (0, 0)),
                pl.BlockSpec((1, slots), lambda i, p: (0, 0)),
                whole,
                whole,
            ],
            out_specs=[vmem()] * 5,
            scratch_shapes=[
                pltpu.VMEM(fresh.shape, BF16),
                pltpu.SemaphoreType.DMA((pieces + 1,)),
            ],
        ),
        out_shape=[
            pltpu.VMEM((rows, streams), BF16),
            pltpu.VMEM((rows, width), BF16),
            pltpu.VMEM((rows, LANES), F32),
            pltpu.VMEM((slots // block, block * cache_len), F32),
            pltpu.VMEM((slots // 2, *cache.shape[1:]), BF16),
        ],
        cost_estimate=cost(1 << 31, 2 * cache.size),
        compiler_params=limit(16),
        name="own_rows",
    )(place, *off_chip(home, active, lengths, fresh, cache))


def attend_kernel(heads, block, pair, count, per_step, *refs):
    part_refs, (bias_ref, early_ref, late_hbm), refs = refs[:count], refs[count:count + 3], refs[count + 3:]
    out_refs, (owned_ref, mixed_ref, got_ref, late_ref, sems) = refs[:-5], refs[-5:]
    rows, _ = got_ref.shape
    slots = owned_ref.shape[0]
    early = early_ref.shape[0]
    cache_len = early_ref.shape[2]
    width = heads * HD
    scale = HD ** (-0.5)
    pieces = sems.shape[0]
    size = late_ref.shape[0] // pieces
    copies = [
        pltpu.make_async_copy(
            late_hbm.at[pl.ds(early + i * size, size)], late_ref.at[pl.ds(i * size, size)], sems.at[i]
        )
        for i in range(pieces)
    ]
    for copy in copies:
        copy.start()

    at = 0
    for part_ref in part_refs:
        got_ref[at:at + part_ref.shape[0]] = part_ref[...]
        at += part_ref.shape[0]
    tail = got_ref[:, width:].astype(F32)
    local = (tail[:, 0:1] * ID_BASE + tail[:, 1:2]).astype(jnp.int32)
    local = jnp.where(tail[:, 2:3] > 0, local, -1)
    hits = lax.broadcasted_iota(jnp.int32, (rows, slots), 1) == local
    matched = jnp.where(hits, 1.0, 0.0).astype(BF16)
    owned_ref[...] = dot(matched, got_ref[:, :width], ((0,), (0,))).astype(BF16)

    span = block * cache_len
    other_slot = jnp.where(
        lax.broadcasted_iota(jnp.int32, (block, span), 0)
        == lax.broadcasted_iota(jnp.int32, (block, span), 1) // cache_len,
        0.0,
        -1e30,
    )
    head_of_row = lax.broadcasted_iota(jnp.int32, (pair * block, pair * HD), 0) // block
    head_of_lane = lax.broadcasted_iota(jnp.int32, (pair * block, pair * HD), 1) // HD
    same_head = head_of_row == head_of_lane
    lanes = lax.broadcasted_iota(jnp.int32, (block, LANES), 1)
    pairs = [slice(j * pair * HD, (j + 1) * pair * HD) for j in range(heads // pair)]

    def cache(start, which, cols):
        ref, at = (early_ref, start) if start < early else (late_ref, start - early)
        return ref[at:at + block, which, :, cols].reshape(span, pair * HD)

    waited = 0
    for first in range(0, slots, block * per_step):
        starts = range(first, first + block * per_step, block)
        while waited < pieces and early + waited * size < starts[-1] + block:
            copies[waited].wait()
            waited += 1
        scores = []
        for start in starts:
            queries = owned_ref[start:start + block, :]
            parts = []
            for cols in pairs:
                query = queries[:, cols]
                spread = jnp.where(same_head, jnp.concatenate([query] * pair, axis=0), 0)
                parts.append(dot(spread.astype(BF16), cache(start, 0, cols), ((1,), (1,))))
            scores.append(jnp.concatenate(parts, axis=0))
        raws, sums, inverses = [], [], []
        for i, start in enumerate(starts):
            hide = other_slot + bias_ref[start // block:start // block + 1, :]
            masked = scores[i] * scale + jnp.concatenate([hide] * heads, axis=0)
            top = jnp.max(masked, axis=1, keepdims=True)
            raw = jnp.exp(masked - top)
            total = jnp.sum(raw, axis=1, keepdims=True)
            raws.append(raw.astype(BF16))
            sums.append(top + jnp.log(total))
            inverses.append(1.0 / total)
        for i, start in enumerate(starts):
            for j, cols in enumerate(pairs):
                tall_rows = slice(j * pair * block, (j + 1) * pair * block)
                mixed = dot(raws[i][tall_rows], cache(start, 1, cols))
                for k in range(pair):
                    h = j * pair + k
                    mixed_ref[start:start + block, h * HD:(h + 1) * HD] = (
                        mixed[k * block:(k + 1) * block, k * HD:(k + 1) * HD]
                        * inverses[i][h * block:(h + 1) * block]
                    ).astype(BF16)
            high = sums[i].astype(BF16).astype(F32)
            middle = (sums[i] - high).astype(BF16).astype(F32)
            low = (sums[i] - high) - middle
            packed = jnp.where(lanes == 3 * heads, 1.0, 0.0)
            for h in range(heads):
                part = slice(h * block, (h + 1) * block)
                packed = jnp.where(lanes == h, high[part], packed)
                packed = jnp.where(lanes == heads + h, middle[part], packed)
                packed = jnp.where(lanes == 2 * heads + h, low[part], packed)
            mixed_ref[start:start + block, width:] = packed.astype(BF16)

    back = dot(matched, mixed_ref[...]).astype(BF16)
    if len(out_refs) == 1:
        out_refs[0][...] = back
        return
    chips, size, _ = out_refs[0].shape
    for k in range(chips):
        for i, out_ref in enumerate(out_refs):
            at = (2 * k + i) * size
            out_ref[k] = back[at:at + size]


def attend(got, early, kv_cache, bias, block, per_step, capacity, chips, pieces=4):
    rows, padded = sum(part.shape[0] for part in got), got[0].shape[1]
    width = padded - LANES
    heads = width // HD
    slots = kv_cache.shape[0]
    late = slots - early.shape[0]
    pair = 2 if heads % 2 == 0 else 1
    if chips:
        outs = [pltpu.VMEM((chips, capacity, padded), BF16)] * 2
    else:
        outs = [pltpu.VMEM((rows, padded), BF16)]
    return pl.pallas_call(
        functools.partial(attend_kernel, heads, block, pair, len(got), per_step),
        in_specs=[vmem()] * (2 + len(got)) + [pl.BlockSpec(memory_space=pl.ANY)],
        out_specs=[vmem()] * len(outs),
        scratch_shapes=[
            pltpu.VMEM((slots, width), BF16),
            pltpu.VMEM((slots, padded), BF16),
            pltpu.VMEM((rows, padded), BF16),
            pltpu.VMEM((late, *kv_cache.shape[1:]), BF16),
            pltpu.SemaphoreType.DMA((pieces,)),
        ],
        out_shape=outs,
        compiler_params=limit(28),
        cost_estimate=cost(4 * rows * slots * padded, 2 * kv_cache.size),
        name="attend",
    )(*on_chip(*got, bias, early), *off_chip(kv_cache))


def pack_kernel(keep_ref, got_ref, *out_refs):
    capacity = keep_ref.shape[1]
    for k, out_ref in enumerate(out_refs):
        out_ref[:capacity] = keep_ref[k]
        out_ref[capacity:] = got_ref[k]


def pack(keep, got):
    chips, capacity, padded = keep.shape
    return pl.pallas_call(
        pack_kernel,
        in_specs=[vmem()] * 2,
        out_specs=[vmem()] * chips,
        out_shape=[pltpu.VMEM((2 * capacity, padded), BF16)] * chips,
        compiler_params=limit(16),
        cost_estimate=cost(1 << 20, 8 * keep.size),
        name="pack",
    )(*on_chip(keep, got))


def merge_kernel(start, count, heads, value_ref, own_ref, *refs):
    back_refs, out_ref = refs[:count], refs[count]
    width = heads * HD
    at = start
    done = 0
    for back_ref in back_refs:
        size = back_ref.shape[0]
        rows = back_ref[...].astype(F32)
        tail = rows[:, width:]
        here = slice(at, at + size)
        own = own_ref[here, :heads]
        log_sum = (tail[:, :heads] + tail[:, heads:2 * heads]) + tail[:, 2 * heads:3 * heads]
        top = jnp.maximum(own, log_sum)
        cached_raw = jnp.exp(log_sum - top)
        own_raw = jnp.exp(own - top)
        total = cached_raw + own_raw
        cached_weight, own_weight = cached_raw / total, own_raw / total
        for h in range(heads):
            cols = slice(h * HD, (h + 1) * HD)
            mixed = cached_weight[:, h:h + 1] * rows[:, cols] + own_weight[:, h:h + 1] * value_ref[
                here, cols
            ].astype(F32)
            out_ref[done:done + size, cols] = mixed.astype(BF16)
        at += size
        done += size


def merge(backs, value, own, start):
    width = value.shape[1]
    size = sum(back.shape[0] for back in backs)
    return pl.pallas_call(
        functools.partial(merge_kernel, start, len(backs), width // HD),
        out_shape=pltpu.VMEM((size, width), BF16),
        in_specs=[vmem()] * (2 + len(backs)),
        out_specs=vmem(),
        cost_estimate=cost(1 << 24, 4 * size * width),
        compiler_params=limit(16),
        name="merge",
    )(*on_chip(value, own, *backs))


def in_stream_order(placing_ref, row_refs):
    total, at = None, 0
    for row_ref in row_refs:
        size = row_ref.shape[0]
        part = dot(placing_ref[at:at + size, :], row_ref[...], ((0,), (0,)))
        total = part if total is None else total + part
        at += size
    return total.astype(BF16)


def own_kernel(count, where_ref, placing_ref, *refs):
    row_refs, (w_ref, residual_ref, out_ref, rows_ref) = refs[:count], refs[count:]
    tile = w_ref.shape[1]

    @pl.when(pl.program_id(0) == 0)
    def _():
        rows_ref[...] = in_stream_order(placing_ref, row_refs)

    cols = pl.ds(pl.multiple_of(pl.program_id(0) * tile, tile), tile)
    out_ref[:, cols] = residual_ref[...].astype(F32) + dot(rows_ref[...], w_ref[...])


def project_own(placing, rows, w_out, residual, place, tile):
    streams, out_cols = residual.shape
    width = w_out.shape[0]
    tiles = out_cols // tile
    return pl.pallas_call(
        functools.partial(own_kernel, len(rows)),
        grid_spec=pltpu.PrefetchScalarGridSpec(
            num_scalar_prefetch=1,
            grid=(tiles,),
            in_specs=[vmem()] * (1 + len(rows))
            + [
                pl.BlockSpec((width, tile), lambda i, p: (0, p[0] * tiles + i)),
                pl.BlockSpec((streams, tile), lambda i, p: (0, i)),
            ],
            out_specs=vmem(),
            scratch_shapes=[pltpu.VMEM((streams, width), BF16)],
        ),
        out_shape=pltpu.VMEM((streams, out_cols), F32),
        cost_estimate=cost(2 * streams * width * out_cols, 2 * width * out_cols),
        compiler_params=limit(16),
        name="project_own",
    )(place, *on_chip(placing, *rows), *off_chip(w_out, residual))


def rest_kernel(rings, count, offsets, where_ref, placing_ref, sum_ref, *refs):
    out_ref, rows_ref = refs[-2:]
    tile = out_ref.shape[1]
    cols = pl.ds(pl.multiple_of(pl.program_id(0) * tile, tile), tile)
    each = len(refs[:-2]) // rings
    pieces = [refs[k * each:(k + 1) * each] for k in range(rings)]

    @pl.when(pl.program_id(0) == 0)
    def _():
        for k, piece in enumerate(pieces):
            rows_ref[k] = in_stream_order(placing_ref, piece[:count])

    total = sum_ref[:, cols]
    for k, piece in enumerate(pieces):
        for offset, w_ref in zip(offsets, piece[count:]):
            size = w_ref.shape[0]
            at = pl.multiple_of(offset(where_ref[1], where_ref[3]), size)
            total += dot(rows_ref[k, :, pl.ds(at, size)], w_ref[:, cols])
    out_ref[...] = total.astype(out_ref.dtype)


def project_rest(placing, partial, pieces, offsets, place, tile, width):
    streams, out_cols = partial.shape
    rings, count = len(pieces), len(pieces[0]) - len(offsets)
    operands = [array for piece in pieces for array in piece]
    return pl.pallas_call(
        functools.partial(rest_kernel, rings, count, offsets),
        grid_spec=pltpu.PrefetchScalarGridSpec(
            num_scalar_prefetch=1,
            grid=(out_cols // tile,),
            in_specs=[vmem()] * (2 + len(operands)),
            out_specs=pl.BlockSpec((streams, tile), lambda i, p: (0, i)),
            scratch_shapes=[pltpu.VMEM((rings, streams, width), BF16)],
        ),
        out_shape=jax.ShapeDtypeStruct((streams, out_cols), BF16),
        cost_estimate=cost(2 * streams * out_cols * 1024, 4 * streams * out_cols),
        compiler_params=limit(16),
        name="project_rest",
    )(place, *on_chip(placing, partial, *operands))


def block_step(residual, fresh_qkv, active, home_slot, kv_cache, lengths, w_out):
    groups = lax.axis_size("dp")
    parts = lax.axis_size("tensor")
    group_here = lax.axis_index("dp")
    part_here = lax.axis_index("tensor")
    streams = home_slot.shape[0]
    width = fresh_qkv.shape[2]
    capacity = max(2, streams // groups)
    padded = width + LANES
    rows = groups * capacity
    tile = min(512, residual.shape[1])
    chips = groups // 2 if capacity % 16 == 0 else 0
    here = group_here if chips else 0
    place = jnp.stack([part_here, group_here % 2, here, group_here // 2 % 2]).astype(jnp.int32)
    swap = [(i, i ^ 1) for i in range(groups)]
    rings = [[(i, (i + k) % parts) for i in range(parts)] for k in range(1, parts)]
    block = 16

    def exchange(sent):
        if not chips:
            sent = sent[0].reshape(groups, capacity, padded)
            sent = lax.all_to_all(sent, "dp", split_axis=0, concat_axis=0, tiled=True)
            return [sent.reshape(rows, padded)]
        keep, give = (half.reshape(chips, capacity, padded) for half in sent)
        packed = pack(keep, lax.ppermute(give, "dp", swap))
        parts = [packed[0]]
        for k in range(1, chips):
            parts.append(lax.ppermute(packed[k], "dp", [(i, i ^ (2 * k)) for i in range(groups)]))
        return parts

    half, unit = width // 2, width // 8
    across = [(i, i ^ 2) for i in range(groups)]
    split = unit % LANES == 0 and groups % 4 == 0
    if split:
        cuts = [
            (lambda core, side: core * half + side * 3 * unit, unit),
            (lambda core, side: core * half + unit, unit),
            (lambda core, side: core * half + 2 * unit, unit),
        ]
        offsets = [cut[0] for cut in cuts]
        offsets.append(lambda core, side: core * half + (1 - side) * 3 * unit)
    else:
        cuts = [(lambda core, side: core * half, half)]
        offsets = [cuts[0][0]]
    flip = [lambda core, side, at=at: at(1 - core, side) for at in offsets]

    home = home_slot.reshape(1, streams)
    live = active.reshape(1, streams)
    fresh = jnp.transpose(fresh_qkv, (1, 0, 2))
    sent, blocks = route(home, live, fresh, w_out, place, capacity, groups, parts, chips, cuts)
    weights = [
        [lax.ppermute(block, "tensor", ring) for block in blocks[i * len(cuts):(i + 1) * len(cuts)]]
        for i, ring in enumerate(rings)
    ]
    placing, value, own, bias, early = own_rows(
        home, live, lengths.reshape(1, -1), fresh, kv_cache, place, capacity, groups, block
    )
    if split:
        for fetched in weights:
            shared, _ = lax.optimization_barrier((fetched[0], bias))
            fetched.append(lax.ppermute(shared, "dp", across))
    got = exchange(sent)
    chunks = exchange(attend(got, early, kv_cache, bias, block, 4, capacity, chips))
    bounds = [chunks[:chips // 2], chunks[chips // 2:]] if chips else [chunks]
    merged, at = [], 0
    for some in bounds:
        merged.append(merge(some, value, own, at))
        at += sum(chunk.shape[0] for chunk in some)
    pieces = []
    for ring, fetched in zip(rings, weights):
        theirs = []
        for part in merged:
            theirs.append(lax.ppermute(part, "tensor", ring))
        *fetched, _ = lax.optimization_barrier((*fetched, merged[0]))
        swapped = [lax.ppermute(some, "dp", swap) for some in fetched]
        pieces.append((*theirs, *fetched, *swapped))
    partial = project_own(placing, merged, w_out, residual, place, tile)
    return project_rest(placing, partial, pieces, offsets + flip, place, tile, width)


def solution(mesh):
    placed = (
        P("dp", "tensor"),
        P("dp", None, "tensor"),
        P("dp"),
        P("dp"),
        P("dp", None, None, "tensor"),
        P("dp"),
        P("tensor", None),
    )
    return jax.shard_map(
        block_step, mesh=mesh, in_specs=placed, out_specs=P("dp", "tensor"), check_vma=False
    )
```

time: 171 us -> 82.4 us (0.48)
  waiting for transfers between devices: 58.5 us -> 16.6 us
  local copies, waits for them, and re-layouts: 34.9 us -> 0 us
  starting transfers between devices: 11.1 us -> 40.5 us
  Pallas kernels: 0 us -> 24.8 us
  matrix products: 24.1 us -> 0 us
  blocking collectives: 23.1 us -> 0 us
  between operations: 13.6 us -> 0.16 us
  other arithmetic: 5.39 us -> 0.08 us
    reduce_scatter x1 -> x0, waiting for transfers between devices: 54.1 us -> none  [body(): lax.psum_scatter(partial_rows, 'tensor', scatter_dimension=1, tiled=True)]
    ppermute x0 -> x26, starting transfers between devices: none -> 40.5 us  [the longest x14 30.3 us: exchange(): lax.ppermute(packed[k], 'dp', [(i, i ^ 2 * k) for i in range(groups)])]
    pallas_call x0 -> x9, Pallas kernels: none -> 24.8 us  [the longest x1 5.21 us: own_rows(): pl.pallas_call(functools.partial(rows_kernel, capacity), grid_spec=pltpu....]
    dot_general x6 -> x0, matrix products: 24.1 us -> none  [the longest x1 7.83 us: body(): jnp.dot(source_rows, w_out, preferred_element_type=jnp.float32)]
    all_to_all x1 -> x0, blocking collectives: 23.1 us -> none  [body(): lax.all_to_all(heads_rows.reshape(groups, capacity, width_here), 'dp', sp...]
    unnamed x8 -> x0, local copies, waits for them, and re-layouts: 19.6 us -> none
    ppermute x0 -> x26, waiting for transfers between devices: none -> 16.6 us  [the longest x14 14.7 us: exchange(): lax.ppermute(packed[k], 'dp', [(i, i ^ 2 * k) for i in range(groups)])]
    slice x1 -> x0, local copies, waits for them, and re-layouts: 12.4 us -> none  [attend_local(): kv_cache[:, 1].reshape(streams_here, cache_len, heads_local, head_size)]
  transfers between devices with their start and end apart: 3 -> 26, of which waited for: 3 -> 6; matrix products, arithmetic and copies ran while one was open for 20% -> 0% of each run, Pallas kernels for 0% -> 21%
where the time goes in v2:
time: 82.4 us; the launch traced here: 82.1 us
  starting transfers between devices  40.5 us (49%)
  Pallas kernels  24.8 us (30%)
  waiting for transfers between devices  16.6 us (20%)
    ppermute x14, starting transfers between devices, exchange(): lax.ppermute(packed[k], 'dp', [(i, i ^ 2 * k) for i in range(groups)])  30.3 us
    ppermute x14, waiting for transfers between devices, exchange(): lax.ppermute(packed[k], 'dp', [(i, i ^ 2 * k) for i in range(groups)])  14.7 us
    pallas_call x1, Pallas kernels, own_rows(): pl.pallas_call(functools.partial(rows_kernel, capacity), grid_spec=pltpu....  5.21 us
    pallas_call x1, Pallas kernels, attend(): pl.pallas_call(functools.partial(attend_kernel, heads, block, pair, len(g...  5.21 us
    pallas_call x1, Pallas kernels, project_own(): pl.pallas_call(functools.partial(own_kernel, len(rows)), grid_spec=pltpu....  5.02 us
    ppermute x3, starting transfers between devices, block_step(): lax.ppermute(block, 'tensor', ring)  4.67 us
    pallas_call x1, Pallas kernels, project_rest(): pl.pallas_call(functools.partial(rest_kernel, rings, count, offsets), gri...  4.59 us
    pallas_call x1, Pallas kernels, route(): pl.pallas_call(functools.partial(route_kernel, capacity, parts, chips, cu...  3.11 us
  transfers between devices with their start and end apart: 26, of which 6 were waited for; matrix products, arithmetic and copies ran while one was open for 0% of the time, Pallas kernels for 21%

profile of v2, /device:TPU:0, one launch (start us, length us, event | category | flops | bytes accessed | tf_op | source)
XLA Modules:
  0.0 82.1 jit_solution(1663543763654536892)
XLA Ops:
  0.0 0.1 pad_add_fusion.place_ref.where_ref
  0.1 3.1 %route.1 = (bf16[128,1152]{1,0:T(8,128)(2,1)S(1)}, bf16[128,1152]{1,0:T(8,128)(2,1)S(1)}, bf16[128,2048]{1,0:T(8,128)(2,1)S(1)}, bf16[128,2048]{1,0:T(8,128)(2,1)S(1)}, bf16[128,2048]{1,0:T(8,128)(2,1)S(1)}) custom-call(s32[4]{0:T(128)S(1)} %pad_add_fusion.place_ref.where_ref, s32[1,256]{1,0:T(1,128)} %bitcast.14, s32[1,256]{1,0:T(1,128)} %bitcast.16, ...), custom_call_target="tpu_custom_call" | custom-call | flops 150994944 | bytes 1048576 | tf_op jit(solution)/shard_map/route/pallas_call | solution.py:112
  3.2 0.6 collective-permute-start
  3.8 2.6 %collective-permute-start.18 = (bf16[128,2048]{1,0:T(8,128)(2,1)S(1)}, bf16[128,2048]{1,0:T(8,128)(2,1)S(1)}, u32[]{:S(2)}, u32[]{:S(2)}) collective-permute-start(bf16[128,2048]{1,0:T(8,128)(2,1)S(1)} %get-tuple-element.63), channel_id=1, source_target_pairs={{0,1},{1,0},{2,3},{3,2},{4,5},{5,4},{6,7},{7,6},{8,9},{9,8},{10,11... | collective-permute-start | bytes 1572872 | tf_op jit(solution)/shard_map/ppermute | solution.py:562
  6.3 0.0 collective-permute-done.got_ref
  6.4 1.6 %collective-permute-start.1 = (bf16[32,1152]{1,0:T(8,128)(2,1)S(1)}, bf16[32,1152]{1,0:T(8,128)(2,1)S(1)}, u32[]{:S(2)}, u32[]{:S(2)}) collective-permute-start(bf16[32,1152]{1,0:T(8,128)(2,1)S(1)} %get-tuple-element.44), channel_id=1, source_target_pairs={{0,4},{2,6},{4,0},{6,2},{8,12},{10,14},{12,8},{14,10},{16,20},{18,... | collective-permute-start | bytes 221192 | tf_op jit(solution)/shard_map/ppermute | solution.py:538
  7.9 1.6 %collective-permute-start.2 = (bf16[32,1152]{1,0:T(8,128)(2,1)S(1)}, bf16[32,1152]{1,0:T(8,128)(2,1)S(1)}, u32[]{:S(2)}, u32[]{:S(2)}) collective-permute-start(bf16[32,1152]{1,0:T(8,128)(2,1)S(1)} %get-tuple-element.45), channel_id=1, source_target_pairs={{0,8},{2,10},{4,12},{6,14},{8,0},{10,2},{12,4},{14,6},{16,24},{18,... | collective-permute-start | bytes 221192 | tf_op jit(solution)/shard_map/ppermute | solution.py:538
  9.5 0.4 collective-permute-start.3
  9.9 2.6 %collective-permute-start.4 = (bf16[32,1152]{1,0:T(8,128)(2,1)S(1)}, bf16[32,1152]{1,0:T(8,128)(2,1)S(1)}, u32[]{:S(2)}, u32[]{:S(2)}) collective-permute-start(bf16[32,1152]{1,0:T(8,128)(2,1)S(1)} %get-tuple-element.47), channel_id=1, source_target_pairs={{0,16},{2,18},{4,20},{6,22},{8,24},{10,26},{12,28},{14,30},{16,0},... | collective-permute-start | bytes 221192 | tf_op jit(solution)/shard_map/ppermute | solution.py:538
  12.5 0.0 collective-permute-done.1.refs_1_
  12.5 1.8 %collective-permute-start.5 = (bf16[32,1152]{1,0:T(8,128)(2,1)S(1)}, bf16[32,1152]{1,0:T(8,128)(2,1)S(1)}, u32[]{:S(2)}, u32[]{:S(2)}) collective-permute-start(bf16[32,1152]{1,0:T(8,128)(2,1)S(1)} %get-tuple-element.48), channel_id=1, source_target_pairs={{0,20},{2,22},{4,16},{6,18},{8,28},{10,30},{12,24},{14,26},{16,4},... | collective-permute-start | bytes 221192 | tf_op jit(solution)/shard_map/ppermute | solution.py:538
  14.3 0.0 collective-permute-done.2.refs_2_
  14.3 3.1 %collective-permute-start.6 = (bf16[32,1152]{1,0:T(8,128)(2,1)S(1)}, bf16[32,1152]{1,0:T(8,128)(2,1)S(1)}, u32[]{:S(2)}, u32[]{:S(2)}) collective-permute-start(bf16[32,1152]{1,0:T(8,128)(2,1)S(1)} %get-tuple-element.49), channel_id=1, source_target_pairs={{0,24},{2,26},{4,28},{6,30},{8,16},{10,18},{12,20},{14,22},{16,8},... | collective-permute-start | bytes 221192 | tf_op jit(solution)/shard_map/ppermute | solution.py:538
  17.4 0.0 collective-permute-done.3.refs_3_
  17.4 1.5 %collective-permute-start.7 = (bf16[32,1152]{1,0:T(8,128)(2,1)S(1)}, bf16[32,1152]{1,0:T(8,128)(2,1)S(1)}, u32[]{:S(2)}, u32[]{:S(2)}) collective-permute-start(bf16[32,1152]{1,0:T(8,128)(2,1)S(1)} %get-tuple-element.50), channel_id=1, source_target_pairs={{0,28},{2,30},{4,24},{6,26},{8,20},{10,22},{12,16},{14,18},{16,12}... | collective-permute-start | bytes 221192 | tf_op jit(solution)/shard_map/ppermute | solution.py:538
  18.9 5.2 %own_rows.1 = (bf16[256,256]{1,0:T(8,128)(2,1)S(1)}, bf16[256,1024]{1,0:T(8,128)(2,1)S(1)}, f32[256,128]{1,0:T(8,128)S(1)}, f32[16,256]{1,0:T(8,128)S(1)}, bf16[128,2,16,1024]{3,2,1,0:T(8,128)(2,1)S(1)}) custom-call(s32[4]{0:T(128)S(1)} %pad_add_fusion.place_ref.where_ref, s32[1,256]{1,0:T(1,128)} %bitcast.15, s32[1,256]{1,0:T(1,128)} %bitcast.17, ...), custom_call_target="tpu_custom_call" | custom-call | flops 2147483648 | bytes 16777216 | tf_op jit(solution)/shard_map/own_rows/pallas_call | solution.py:198
  24.1 0.0 collective-permute-done.4.refs_4_
  24.1 0.5 collective-permute-done.5.refs_5_
  24.6 0.0 collective-permute-done.6.refs_6_
  24.6 0.0 collective-permute-done.7.refs_7_
  24.6 5.2 %attend.1 = (bf16[8,16,1152]{2,1,0:T(8,128)(2,1)S(1)}, bf16[8,16,1152]{2,1,0:T(8,128)(2,1)S(1)}) custom-call(bf16[32,1152]{1,0:T(8,128)(2,1)S(1)} %get-tuple-element.43.refs_0_, bf16[32,1152]{1,0:T(8,128)(2,1)S(1)} %collective-permute-done.1.refs_1_, bf16[32,1152]{1,0:T(8,128)(2,1)S(1)} %collective-permute-done.2.refs_2_, ...), custom_call_target="tpu_custom_call" | custom-call | flops 301989888 | bytes 16777216 | tf_op jit(solution)/shard_map/attend/pallas_call | solution.py:345
  29.8 0.1 collective-permute-start.8
  29.9 1.6 %collective-permute-start.19 = (bf16[128,2048]{1,0:T(8,128)(2,1)S(1)}, bf16[128,2048]{1,0:T(8,128)(2,1)S(1)}, u32[]{:S(2)}, u32[]{:S(2)}) collective-permute-start(bf16[128,2048]{1,0:T(8,128)(2,1)S(1)} %get-tuple-element.64), channel_id=1, source_target_pairs={{0,1},{1,0},{2,3},{3,2},{4,5},{5,4},{6,7},{7,6},{8,9},{9,8},{10,11... | collective-permute-start | bytes 1572872 | tf_op jit(solution)/shard_map/ppermute | solution.py:562
  31.5 0.5 collective-permute-start.20
  32.0 0.0 collective-permute-done.18.refs_2_
  32.0 0.7 collective-permute-start.21
  32.8 0.0 collective-permute-done.8.got_ref
  32.8 1.4 %collective-permute-start.9 = (bf16[32,1152]{1,0:T(8,128)(2,1)S(1)}, bf16[32,1152]{1,0:T(8,128)(2,1)S(1)}, u32[]{:S(2)}, u32[]{:S(2)}) collective-permute-start(bf16[32,1152]{1,0:T(8,128)(2,1)S(1)} %get-tuple-element.56), channel_id=1, source_target_pairs={{0,4},{2,6},{4,0},{6,2},{8,12},{10,14},{12,8},{14,10},{16,20},{18,... | collective-permute-start | bytes 221192 | tf_op jit(solution)/shard_map/ppermute | solution.py:538
  34.2 4.3 %collective-permute-start.12 = (bf16[32,1152]{1,0:T(8,128)(2,1)S(1)}, bf16[32,1152]{1,0:T(8,128)(2,1)S(1)}, u32[]{:S(2)}, u32[]{:S(2)}) collective-permute-start(bf16[32,1152]{1,0:T(8,128)(2,1)S(1)} %get-tuple-element.59), channel_id=1, source_target_pairs={{0,16},{2,18},{4,20},{6,22},{8,24},{10,26},{12,28},{14,30},{16,0},... | collective-permute-start | bytes 221192 | tf_op jit(solution)/shard_map/ppermute | solution.py:538
  38.5 8.8 %collective-permute-done.9.refs_1_ = bf16[32,1152]{1,0:T(8,128)(2,1)S(1)} collective-permute-done((bf16[32,1152]{1,0:T(8,128)(2,1)S(1)}, bf16[32,1152]{1,0:T(8,128)(2,1)S(1)}, u32[]{:S(2)}, u32[]{:S(2)}) %collective-permute-start.9) | collective-permute-done | bytes 73760 | tf_op jit(solution)/shard_map/ppermute | solution.py:538
  47.3 4.3 %collective-permute-start.13 = (bf16[32,1152]{1,0:T(8,128)(2,1)S(1)}, bf16[32,1152]{1,0:T(8,128)(2,1)S(1)}, u32[]{:S(2)}, u32[]{:S(2)}) collective-permute-start(bf16[32,1152]{1,0:T(8,128)(2,1)S(1)} %get-tuple-element.60), channel_id=1, source_target_pairs={{0,20},{2,22},{4,16},{6,18},{8,28},{10,30},{12,24},{14,26},{16,4},... | collective-permute-start | bytes 221192 | tf_op jit(solution)/shard_map/ppermute | solution.py:538
  51.6 0.0 collective-permute-done.12.refs_0_
  51.6 1.5 %collective-permute-start.14 = (bf16[32,1152]{1,0:T(8,128)(2,1)S(1)}, bf16[32,1152]{1,0:T(8,128)(2,1)S(1)}, u32[]{:S(2)}, u32[]{:S(2)}) collective-permute-start(bf16[32,1152]{1,0:T(8,128)(2,1)S(1)} %get-tuple-element.61), channel_id=1, source_target_pairs={{0,24},{2,26},{4,28},{6,30},{8,16},{10,18},{12,20},{14,22},{16,8},... | collective-permute-start | bytes 221192 | tf_op jit(solution)/shard_map/ppermute | solution.py:538
  53.1 1.6 %collective-permute-done.13.refs_1_ = bf16[32,1152]{1,0:T(8,128)(2,1)S(1)} collective-permute-done((bf16[32,1152]{1,0:T(8,128)(2,1)S(1)}, bf16[32,1152]{1,0:T(8,128)(2,1)S(1)}, u32[]{:S(2)}, u32[]{:S(2)}) %collective-permute-start.13) | collective-permute-done | bytes 73760 | tf_op jit(solution)/shard_map/ppermute | solution.py:538
  54.7 4.2 %collective-permute-start.15 = (bf16[32,1152]{1,0:T(8,128)(2,1)S(1)}, bf16[32,1152]{1,0:T(8,128)(2,1)S(1)}, u32[]{:S(2)}, u32[]{:S(2)}) collective-permute-start(bf16[32,1152]{1,0:T(8,128)(2,1)S(1)} %get-tuple-element.62), channel_id=1, source_target_pairs={{0,28},{2,30},{4,24},{6,26},{8,20},{10,22},{12,16},{14,18},{16,12}... | collective-permute-start | bytes 221192 | tf_op jit(solution)/shard_map/ppermute | solution.py:538
  59.0 0.0 collective-permute-done.14.refs_2_
  59.0 0.3 collective-permute-start.10
  59.3 2.6 %collective-permute-done.15.refs_3_ = bf16[32,1152]{1,0:T(8,128)(2,1)S(1)} collective-permute-done((bf16[32,1152]{1,0:T(8,128)(2,1)S(1)}, bf16[32,1152]{1,0:T(8,128)(2,1)S(1)}, u32[]{:S(2)}, u32[]{:S(2)}) %collective-permute-start.15) | collective-permute-done | bytes 73760 | tf_op jit(solution)/shard_map/ppermute | solution.py:538
  61.9 1.8 %collective-permute-start.11 = (bf16[32,1152]{1,0:T(8,128)(2,1)S(1)}, bf16[32,1152]{1,0:T(8,128)(2,1)S(1)}, u32[]{:S(2)}, u32[]{:S(2)}) collective-permute-start(bf16[32,1152]{1,0:T(8,128)(2,1)S(1)} %get-tuple-element.58), channel_id=1, source_target_pairs={{0,12},{2,14},{4,8},{6,10},{8,4},{10,6},{12,0},{14,2},{16,28},{18,... | collective-permute-start | bytes 221192 | tf_op jit(solution)/shard_map/ppermute | solution.py:538
  63.7 0.8 merge.3.refs_1_
  64.5 0.0 collective-permute-done.10.refs_2_
  64.5 1.6 %collective-permute-start.17 = (bf16[128,1024]{1,0:T(8,128)(2,1)S(1)}, bf16[128,1024]{1,0:T(8,128)(2,1)S(1)}, u32[]{:S(2)}, u32[]{:S(2)}) collective-permute-start(bf16[128,1024]{1,0:T(8,128)(2,1)S(1)} %merge.3.refs_1_), channel_id=1, source_target_pairs={{0,1},{1,0},{2,3},{3,2},{4,5},{5,4},{6,7},{7,6},{8,9},{9,8},{10,11... | collective-permute-start | bytes 786440 | tf_op jit(solution)/shard_map/ppermute | solution.py:583
  66.1 1.1 %collective-permute-done.11.refs_3_ = bf16[32,1152]{1,0:T(8,128)(2,1)S(1)} collective-permute-done((bf16[32,1152]{1,0:T(8,128)(2,1)S(1)}, bf16[32,1152]{1,0:T(8,128)(2,1)S(1)}, u32[]{:S(2)}, u32[]{:S(2)}) %collective-permute-start.11) | collective-permute-done | bytes 73760 | tf_op jit(solution)/shard_map/ppermute | solution.py:538
  67.2 0.8 merge.2.refs_0_
  67.9 0.0 collective-permute-done.19.refs_3_
  67.9 0.0 collective-permute-done.20.refs_4_
  67.9 0.0 collective-permute-done.21.refs_5_
  68.0 0.1 collective-permute-start.22
  68.0 0.5 collective-permute-start.23
  68.5 0.1 collective-permute-start.24
  68.6 0.4 collective-permute-start.25
  69.0 1.9 %collective-permute-done.17.refs_1_ = bf16[128,1024]{1,0:T(8,128)(2,1)S(1)} collective-permute-done((bf16[128,1024]{1,0:T(8,128)(2,1)S(1)}, bf16[128,1024]{1,0:T(8,128)(2,1)S(1)}, u32[]{:S(2)}, u32[]{:S(2)}) %collective-permute-start.17) | collective-permute-done | bytes 262176 | tf_op jit(solution)/shard_map/ppermute | solution.py:583
  71.0 1.5 %collective-permute-start.16 = (bf16[128,1024]{1,0:T(8,128)(2,1)S(1)}, bf16[128,1024]{1,0:T(8,128)(2,1)S(1)}, u32[]{:S(2)}, u32[]{:S(2)}) collective-permute-start(bf16[128,1024]{1,0:T(8,128)(2,1)S(1)} %merge.2.refs_0_), channel_id=1, source_target_pairs={{0,1},{1,0},{2,3},{3,2},{4,5},{5,4},{6,7},{7,6},{8,9},{9,8},{10,11... | collective-permute-start | bytes 786440 | tf_op jit(solution)/shard_map/ppermute | solution.py:583
  72.5 5.0 %project_own.1.sum_ref = f32[256,2048]{1,0:T(8,128)S(1)} custom-call(s32[4]{0:T(128)S(1)} %pad_add_fusion.place_ref.where_ref, bf16[256,256]{1,0:T(8,128)(2,1)S(1)} %get-tuple-element.38.placing_ref, bf16[128,1024]{1,0:T(8,128)(2,1)S(1)} %merge.2.refs_0_, bf16[128,1024]{1,0:T(8,128)(2,1)S(1)} %merge.3.refs_1_, bf16[1024,4096]{1,0:T(8,128)(2,1)} %refs_2_.1, ...), custom_call_target="tpu_custom_call" | custom-call | flops 1073741824 | bytes 4194304 | tf_op jit(solution)/shard_map/project_own/pallas_call | solution.py:450
  77.5 0.0 collective-permute-done.16.refs_0_
  77.5 0.0 collective-permute-done.22.refs_6_
  77.5 0.0 collective-permute-done.23.refs_7_
  77.5 0.0 collective-permute-done.24.refs_8_
  77.5 0.0 collective-permute-done.25.refs_9_
  77.5 4.6 %project_rest.1 = bf16[256,2048]{1,0:T(8,128)(2,1)} custom-call(s32[4]{0:T(128)S(1)} %pad_add_fusion.place_ref.where_ref, bf16[256,256]{1,0:T(8,128)(2,1)S(1)} %get-tuple-element.38.placing_ref, f32[256,2048]{1,0:T(8,128)S(1)} %project_own.1.sum_ref, bf16[128,1024]{1,0:T(8,128)(2,1)S(1)} %collective-permute-done.16.refs_0_, ...), custom_call_target="tpu_custom_call" | custom-call | flops 1073741824 | bytes 2097152 | tf_op jit(solution)/shard_map/project_rest/pallas_call | solution.py:495
  (2 shorter events, 0.1 us)
Async XLA Ops:
  3.2 3.1 %collective-permute-start = (bf16[8,16,1152]{2,1,0:T(8,128)(2,1)S(1)}, bf16[8,16,1152]{2,1,0:T(8,128)(2,1)S(1)}, u32[]{:S(2)}, u32[]{:S(2)}) collective-permute-start(bf16[8,16,1152]{2,1,0:T(8,128)(2,1)S(1)} %bitcast.11), channel_id=1, source_target_pairs={{0,2},{2,0},{4,6},{6,4},{8,10},{10,8},{12,14},{14,12},{16,18},{18,... | collective-permute-start | bytes 884744 | tf_op jit(solution)/shard_map/ppermute | solution.py:535
  3.8 28.3 %collective-permute-start.18 = (bf16[128,2048]{1,0:T(8,128)(2,1)S(1)}, bf16[128,2048]{1,0:T(8,128)(2,1)S(1)}, u32[]{:S(2)}, u32[]{:S(2)}) collective-permute-start(bf16[128,2048]{1,0:T(8,128)(2,1)S(1)} %get-tuple-element.63), channel_id=1, source_target_pairs={{0,1},{1,0},{2,3},{3,2},{4,5},{5,4},{6,7},{7,6},{8,9},{9,8},{10,11... | collective-permute-start | bytes 1572872 | tf_op jit(solution)/shard_map/ppermute | solution.py:562
  6.4 6.1 %collective-permute-start.1 = (bf16[32,1152]{1,0:T(8,128)(2,1)S(1)}, bf16[32,1152]{1,0:T(8,128)(2,1)S(1)}, u32[]{:S(2)}, u32[]{:S(2)}) collective-permute-start(bf16[32,1152]{1,0:T(8,128)(2,1)S(1)} %get-tuple-element.44), channel_id=1, source_target_pairs={{0,4},{2,6},{4,0},{6,2},{8,12},{10,14},{12,8},{14,10},{16,20},{18,... | collective-permute-start | bytes 221192 | tf_op jit(solution)/shard_map/ppermute | solution.py:538
  7.9 6.4 %collective-permute-start.2 = (bf16[32,1152]{1,0:T(8,128)(2,1)S(1)}, bf16[32,1152]{1,0:T(8,128)(2,1)S(1)}, u32[]{:S(2)}, u32[]{:S(2)}) collective-permute-start(bf16[32,1152]{1,0:T(8,128)(2,1)S(1)} %get-tuple-element.45), channel_id=1, source_target_pairs={{0,8},{2,10},{4,12},{6,14},{8,0},{10,2},{12,4},{14,6},{16,24},{18,... | collective-permute-start | bytes 221192 | tf_op jit(solution)/shard_map/ppermute | solution.py:538
  9.5 7.9 %collective-permute-start.3 = (bf16[32,1152]{1,0:T(8,128)(2,1)S(1)}, bf16[32,1152]{1,0:T(8,128)(2,1)S(1)}, u32[]{:S(2)}, u32[]{:S(2)}) collective-permute-start(bf16[32,1152]{1,0:T(8,128)(2,1)S(1)} %get-tuple-element.46), channel_id=1, source_target_pairs={{0,12},{2,14},{4,8},{6,10},{8,4},{10,6},{12,0},{14,2},{16,28},{18,... | collective-permute-start | bytes 221192 | tf_op jit(solution)/shard_map/ppermute | solution.py:538
  9.9 14.1 %collective-permute-start.4 = (bf16[32,1152]{1,0:T(8,128)(2,1)S(1)}, bf16[32,1152]{1,0:T(8,128)(2,1)S(1)}, u32[]{:S(2)}, u32[]{:S(2)}) collective-permute-start(bf16[32,1152]{1,0:T(8,128)(2,1)S(1)} %get-tuple-element.47), channel_id=1, source_target_pairs={{0,16},{2,18},{4,20},{6,22},{8,24},{10,26},{12,28},{14,30},{16,0},... | collective-permute-start | bytes 221192 | tf_op jit(solution)/shard_map/ppermute | solution.py:538
  12.5 12.1 %collective-permute-start.5 = (bf16[32,1152]{1,0:T(8,128)(2,1)S(1)}, bf16[32,1152]{1,0:T(8,128)(2,1)S(1)}, u32[]{:S(2)}, u32[]{:S(2)}) collective-permute-start(bf16[32,1152]{1,0:T(8,128)(2,1)S(1)} %get-tuple-element.48), channel_id=1, source_target_pairs={{0,20},{2,22},{4,16},{6,18},{8,28},{10,30},{12,24},{14,26},{16,4},... | collective-permute-start | bytes 221192 | tf_op jit(solution)/shard_map/ppermute | solution.py:538
  14.3 10.3 %collective-permute-start.6 = (bf16[32,1152]{1,0:T(8,128)(2,1)S(1)}, bf16[32,1152]{1,0:T(8,128)(2,1)S(1)}, u32[]{:S(2)}, u32[]{:S(2)}) collective-permute-start(bf16[32,1152]{1,0:T(8,128)(2,1)S(1)} %get-tuple-element.49), channel_id=1, source_target_pairs={{0,24},{2,26},{4,28},{6,30},{8,16},{10,18},{12,20},{14,22},{16,8},... | collective-permute-start | bytes 221192 | tf_op jit(solution)/shard_map/ppermute | solution.py:538
  17.4 7.2 %collective-permute-start.7 = (bf16[32,1152]{1,0:T(8,128)(2,1)S(1)}, bf16[32,1152]{1,0:T(8,128)(2,1)S(1)}, u32[]{:S(2)}, u32[]{:S(2)}) collective-permute-start(bf16[32,1152]{1,0:T(8,128)(2,1)S(1)} %get-tuple-element.50), channel_id=1, source_target_pairs={{0,28},{2,30},{4,24},{6,26},{8,20},{10,22},{12,16},{14,18},{16,12}... | collective-permute-start | bytes 221192 | tf_op jit(solution)/shard_map/ppermute | solution.py:538
  29.8 2.9 %collective-permute-start.8 = (bf16[8,16,1152]{2,1,0:T(8,128)(2,1)S(1)}, bf16[8,16,1152]{2,1,0:T(8,128)(2,1)S(1)}, u32[]{:S(2)}, u32[]{:S(2)}) collective-permute-start(bf16[8,16,1152]{2,1,0:T(8,128)(2,1)S(1)} %get-tuple-element.54), channel_id=1, source_target_pairs={{0,2},{2,0},{4,6},{6,4},{8,10},{10,8},{12,14},{14,12},{16,18},{18,... | collective-permute-start | bytes 884744 | tf_op jit(solution)/shard_map/ppermute | solution.py:535
  29.9 38.0 %collective-permute-start.19 = (bf16[128,2048]{1,0:T(8,128)(2,1)S(1)}, bf16[128,2048]{1,0:T(8,128)(2,1)S(1)}, u32[]{:S(2)}, u32[]{:S(2)}) collective-permute-start(bf16[128,2048]{1,0:T(8,128)(2,1)S(1)} %get-tuple-element.64), channel_id=1, source_target_pairs={{0,1},{1,0},{2,3},{3,2},{4,5},{5,4},{6,7},{7,6},{8,9},{9,8},{10,11... | collective-permute-start | bytes 1572872 | tf_op jit(solution)/shard_map/ppermute | solution.py:562
  31.5 36.4 %collective-permute-start.20 = (bf16[128,2048]{1,0:T(8,128)(2,1)S(1)}, bf16[128,2048]{1,0:T(8,128)(2,1)S(1)}, u32[]{:S(2)}, u32[]{:S(2)}) collective-permute-start(bf16[128,2048]{1,0:T(8,128)(2,1)S(1)} %get-tuple-element.65), channel_id=1, source_target_pairs={{0,1},{1,0},{2,3},{3,2},{4,5},{5,4},{6,7},{7,6},{8,9},{9,8},{10,11... | collective-permute-start | bytes 1572872 | tf_op jit(solution)/shard_map/ppermute | solution.py:562
  32.0 35.9 %collective-permute-start.21 = (bf16[128,2048]{1,0:T(8,128)(2,1)S(1)}, bf16[128,2048]{1,0:T(8,128)(2,1)S(1)}, u32[]{:S(2)}, u32[]{:S(2)}) collective-permute-start(bf16[128,2048]{1,0:T(8,128)(2,1)S(1)} %collective-permute-done.18.refs_2_), channel_id=1, source_target_pairs={{0,4},{2,6},{4,0},{6,2},{8,12},{10,14},{12,8},{14,10},{16,20},{18,... | collective-permute-start | bytes 1572872 | tf_op jit(solution)/shard_map/ppermute | solution.py:571
  32.8 14.5 %collective-permute-start.9 = (bf16[32,1152]{1,0:T(8,128)(2,1)S(1)}, bf16[32,1152]{1,0:T(8,128)(2,1)S(1)}, u32[]{:S(2)}, u32[]{:S(2)}) collective-permute-start(bf16[32,1152]{1,0:T(8,128)(2,1)S(1)} %get-tuple-element.56), channel_id=1, source_target_pairs={{0,4},{2,6},{4,0},{6,2},{8,12},{10,14},{12,8},{14,10},{16,20},{18,... | collective-permute-start | bytes 221192 | tf_op jit(solution)/shard_map/ppermute | solution.py:538
  34.2 17.5 %collective-permute-start.12 = (bf16[32,1152]{1,0:T(8,128)(2,1)S(1)}, bf16[32,1152]{1,0:T(8,128)(2,1)S(1)}, u32[]{:S(2)}, u32[]{:S(2)}) collective-permute-start(bf16[32,1152]{1,0:T(8,128)(2,1)S(1)} %get-tuple-element.59), channel_id=1, source_target_pairs={{0,16},{2,18},{4,20},{6,22},{8,24},{10,26},{12,28},{14,30},{16,0},... | collective-permute-start | bytes 221192 | tf_op jit(solution)/shard_map/ppermute | solution.py:538
  47.3 7.4 %collective-permute-start.13 = (bf16[32,1152]{1,0:T(8,128)(2,1)S(1)}, bf16[32,1152]{1,0:T(8,128)(2,1)S(1)}, u32[]{:S(2)}, u32[]{:S(2)}) collective-permute-start(bf16[32,1152]{1,0:T(8,128)(2,1)S(1)} %get-tuple-element.60), channel_id=1, source_target_pairs={{0,20},{2,22},{4,16},{6,18},{8,28},{10,30},{12,24},{14,26},{16,4},... | collective-permute-start | bytes 221192 | tf_op jit(solution)/shard_map/ppermute | solution.py:538
  51.6 7.4 %collective-permute-start.14 = (bf16[32,1152]{1,0:T(8,128)(2,1)S(1)}, bf16[32,1152]{1,0:T(8,128)(2,1)S(1)}, u32[]{:S(2)}, u32[]{:S(2)}) collective-permute-start(bf16[32,1152]{1,0:T(8,128)(2,1)S(1)} %get-tuple-element.61), channel_id=1, source_target_pairs={{0,24},{2,26},{4,28},{6,30},{8,16},{10,18},{12,20},{14,22},{16,8},... | collective-permute-start | bytes 221192 | tf_op jit(solution)/shard_map/ppermute | solution.py:538
  54.7 7.2 %collective-permute-start.15 = (bf16[32,1152]{1,0:T(8,128)(2,1)S(1)}, bf16[32,1152]{1,0:T(8,128)(2,1)S(1)}, u32[]{:S(2)}, u32[]{:S(2)}) collective-permute-start(bf16[32,1152]{1,0:T(8,128)(2,1)S(1)} %get-tuple-element.62), channel_id=1, source_target_pairs={{0,28},{2,30},{4,24},{6,26},{8,20},{10,22},{12,16},{14,18},{16,12}... | collective-permute-start | bytes 221192 | tf_op jit(solution)/shard_map/ppermute | solution.py:538
  59.0 5.5 %collective-permute-start.10 = (bf16[32,1152]{1,0:T(8,128)(2,1)S(1)}, bf16[32,1152]{1,0:T(8,128)(2,1)S(1)}, u32[]{:S(2)}, u32[]{:S(2)}) collective-permute-start(bf16[32,1152]{1,0:T(8,128)(2,1)S(1)} %get-tuple-element.57), channel_id=1, source_target_pairs={{0,8},{2,10},{4,12},{6,14},{8,0},{10,2},{12,4},{14,6},{16,24},{18,... | collective-permute-start | bytes 221192 | tf_op jit(solution)/shard_map/ppermute | solution.py:538
  61.9 5.3 %collective-permute-start.11 = (bf16[32,1152]{1,0:T(8,128)(2,1)S(1)}, bf16[32,1152]{1,0:T(8,128)(2,1)S(1)}, u32[]{:S(2)}, u32[]{:S(2)}) collective-permute-start(bf16[32,1152]{1,0:T(8,128)(2,1)S(1)} %get-tuple-element.58), channel_id=1, source_target_pairs={{0,12},{2,14},{4,8},{6,10},{8,4},{10,6},{12,0},{14,2},{16,28},{18,... | collective-permute-start | bytes 221192 | tf_op jit(solution)/shard_map/ppermute | solution.py:538
  64.5 6.4 %collective-permute-start.17 = (bf16[128,1024]{1,0:T(8,128)(2,1)S(1)}, bf16[128,1024]{1,0:T(8,128)(2,1)S(1)}, u32[]{:S(2)}, u32[]{:S(2)}) collective-permute-start(bf16[128,1024]{1,0:T(8,128)(2,1)S(1)} %merge.3.refs_1_), channel_id=1, source_target_pairs={{0,1},{1,0},{2,3},{3,2},{4,5},{5,4},{6,7},{7,6},{8,9},{9,8},{10,11... | collective-permute-start | bytes 786440 | tf_op jit(solution)/shard_map/ppermute | solution.py:583
  68.0 9.5 %collective-permute-start.22 = (bf16[128,2048]{1,0:T(8,128)(2,1)S(1)}, bf16[128,2048]{1,0:T(8,128)(2,1)S(1)}, u32[]{:S(2)}, u32[]{:S(2)}) collective-permute-start(bf16[128,2048]{1,0:T(8,128)(2,1)S(1)} %collective-permute-done.18.refs_2_), channel_id=1, source_target_pairs={{0,2},{2,0},{4,6},{6,4},{8,10},{10,8},{12,14},{14,12},{16,18},{18,... | collective-permute-start | bytes 1572872 | tf_op jit(solution)/shard_map/ppermute | solution.py:585
  68.0 9.5 %collective-permute-start.23 = (bf16[128,2048]{1,0:T(8,128)(2,1)S(1)}, bf16[128,2048]{1,0:T(8,128)(2,1)S(1)}, u32[]{:S(2)}, u32[]{:S(2)}) collective-permute-start(bf16[128,2048]{1,0:T(8,128)(2,1)S(1)} %collective-permute-done.19.refs_3_), channel_id=1, source_target_pairs={{0,2},{2,0},{4,6},{6,4},{8,10},{10,8},{12,14},{14,12},{16,18},{18,... | collective-permute-start | bytes 1572872 | tf_op jit(solution)/shard_map/ppermute | solution.py:585
  68.5 9.0 %collective-permute-start.24 = (bf16[128,2048]{1,0:T(8,128)(2,1)S(1)}, bf16[128,2048]{1,0:T(8,128)(2,1)S(1)}, u32[]{:S(2)}, u32[]{:S(2)}) collective-permute-start(bf16[128,2048]{1,0:T(8,128)(2,1)S(1)} %collective-permute-done.20.refs_4_), channel_id=1, source_target_pairs={{0,2},{2,0},{4,6},{6,4},{8,10},{10,8},{12,14},{14,12},{16,18},{18,... | collective-permute-start | bytes 1572872 | tf_op jit(solution)/shard_map/ppermute | solution.py:585
  68.6 8.9 %collective-permute-start.25 = (bf16[128,2048]{1,0:T(8,128)(2,1)S(1)}, bf16[128,2048]{1,0:T(8,128)(2,1)S(1)}, u32[]{:S(2)}, u32[]{:S(2)}) collective-permute-start(bf16[128,2048]{1,0:T(8,128)(2,1)S(1)} %collective-permute-done.21.refs_5_), channel_id=1, source_target_pairs={{0,2},{2,0},{4,6},{6,4},{8,10},{10,8},{12,14},{14,12},{16,18},{18,... | collective-permute-start | bytes 1572872 | tf_op jit(solution)/shard_map/ppermute | solution.py:585
  71.0 6.5 %collective-permute-start.16 = (bf16[128,1024]{1,0:T(8,128)(2,1)S(1)}, bf16[128,1024]{1,0:T(8,128)(2,1)S(1)}, u32[]{:S(2)}, u32[]{:S(2)}) collective-permute-start(bf16[128,1024]{1,0:T(8,128)(2,1)S(1)} %merge.2.refs_0_), channel_id=1, source_target_pairs={{0,1},{1,0},{2,3},{3,2},{4,5},{5,4},{6,7},{7,6},{8,9},{9,8},{10,11... | collective-permute-start | bytes 786440 | tf_op jit(solution)/shard_map/ppermute | solution.py:583
